TPU v7x, 32 devices: a whole 2x2x4 slice. The times are simulated.
32 devices in a mesh: rep: 2 (over x), dp: 16 (over y, z, core).
Axes of the slice: x: 2, y: 2, z: 4, core: 2. Of those that a mesh axis runs over, the one named last changes fastest.
Arguments:
- x: bfloat16 [32, 1024, 512], P(('rep', 'dp')), parts along dimension 0
- dy: bfloat16 [32, 1024, 512], P(('rep', 'dp')), parts along dimension 0
- w_gate: bfloat16 [2, 512, 8192], P(None, 'dp')
- w_up: bfloat16 [2, 512, 8192], P(None, 'dp')
- w_down: bfloat16 [2, 8192, 512], P(None, 'dp')
Outputs:
- output 1: bfloat16 [32, 1024, 512], P(('rep', 'dp')), parts along dimension 0
- output 2: bfloat16 [4, 512, 8192], P('rep', 'dp'), parts along dimension 0
- output 3: bfloat16 [4, 512, 8192], P('rep', 'dp'), parts along dimension 0
- output 4: bfloat16 [4, 8192, 512], P('rep', 'dp'), parts along dimension 0
There are 2 independent parts. A program takes and returns all parts, laid end to end along the dimension named above; an argument that names none is the same for every part.
All inputs are finite; a program needn't handle non-finite values.
Results may differ from a plain program's by a relative error of at most 0.018.
Values are sent between devices in bfloat16 or wider.
A program may use at most 2 GiB of HBM per device.

v0:
```python
import jax
import jax.numpy as jnp
from jax import lax

NAMES = ("w_gate", "w_up", "w_down")


def matmul(a, w):
    return jnp.dot(a, w, preferred_element_type=jnp.float32).astype(jnp.bfloat16)


def normed(h):
    wide = h.astype(jnp.float32)
    scale = lax.rsqrt(jnp.mean(wide**2, -1, keepdims=True) + 1e-6)
    return (wide * scale).astype(jnp.bfloat16)


def layer(h, w):
    a = normed(h)
    gate = jnp.dot(a, w["w_gate"], preferred_element_type=jnp.float32)
    up = jnp.dot(a, w["w_up"], preferred_element_type=jnp.float32)
    return h + matmul((jax.nn.silu(gate) * up).astype(jnp.bfloat16), w["w_down"])


def stack(weights, h):
    for number in range(weights["w_gate"].shape[0]):
        h = layer(h, {name: w[number] for name, w in weights.items()})
    return h


def solution(mesh):
    groups = mesh.shape["rep"]

    def step(x, dy, *weights):
        shape = x.shape
        x, dy = (t.reshape(groups, -1, *t.shape[1:]) for t in (x, dy))

        def of_a_group(x, dy):
            _, back = jax.vjp(stack, dict(zip(NAMES, weights, strict=True)), x)
            by_weights, by_x = back(dy)
            return (by_x, *(by_weights[name] for name in NAMES))

        by_x, *by_weights = jax.vmap(of_a_group)(x, dy)
        return (by_x.reshape(shape), *(t.reshape(-1, *t.shape[2:]) for t in by_weights))

    return step
```

profile of v0, /device:TPU:0, one launch (start us, length us, event | category | flops | bytes accessed | tf_op | source)
XLA Modules:
  0.0 1642.3 jit_solution(13274915426617950321)
XLA Ops:
  7.2 2.3 fusion.141
  9.5 0.0 all-gather.32.cloned.1.call-start
  9.6 2.2 fusion.140
  11.8 0.0 all-gather.34.cloned.1.call-start
  11.9 2.3 fusion.139
  14.3 0.5 all-gather.36.cloned.1.call-update
  14.8 0.5 all-gather.40.cloned.1.call-update
  15.4 0.5 all-gather.38.cloned.1.call-update
  16.0 1.5 fusion.59
  17.5 1.5 copy.1
  19.0 0.6 multiply_add_fusion.1
  19.6 2.3 copy
  21.9 65.6 %all-gather.30.cloned.1.call-done = bf16[1,512,8192]{2,1,0:T(8,128)(2,1)} async-done(((bf16[1,32,8192]{2,1,0:T(8,128)(2,1)}), bf16[1,512,8192]{2,1,0:T(8,128)(2,1)}) %all-gather.30.cloned.1.call-update) | async-done | bytes 8388624 | tf_op jit(solution)/vmap(jvp())/squeeze | solution.py:27
  87.5 19.0 %fusion.57 = f32[1024,8192]{1,0:T(8,128)} fusion(bf16[1,512,8192]{2,1,0:T(8,128)(2,1)} %all-gather.30.cloned.1.call-done, bf16[1,1024,512]{2,1,0:T(8,128)(2,1)} %param.1, f32[1024]{0:T(1024)S(1)} %get-tuple-element.13), kind=kOutput, calls=%fused_computation.65 | convolution fusion | flops 8591507456 | bytes 42995712 | tf_op jit(solution)/vmap(jvp())/dot_general | solution.py:20
  106.5 56.5 %all-gather.32.cloned.1.call-done = bf16[1,512,8192]{2,1,0:T(8,128)(2,1)} async-done(((bf16[1,32,8192]{2,1,0:T(8,128)(2,1)}), bf16[1,512,8192]{2,1,0:T(8,128)(2,1)}) %all-gather.32.cloned.1.call-update) | async-done | bytes 8388624 | tf_op jit(solution)/vmap(jvp())/squeeze | solution.py:27
  163.0 17.9 %fusion.53 = f32[1024,8192]{1,0:T(8,128)} fusion(bf16[1,512,8192]{2,1,0:T(8,128)(2,1)} %all-gather.32.cloned.1.call-done, bf16[1,1024,512]{2,1,0:T(8,128)(2,1)S(1)} %copy-done.4, f32[1024]{0:T(1024)S(1)} %get-tuple-element.13), kind=kOutput, calls=%fused_computation.61 | convolution fusion | flops 8591507456 | bytes 42995712 | tf_op jit(solution)/vmap(jvp())/dot_general | solution.py:21
  180.9 27.4 %fusion.24 = bf16[1024,8192]{1,0:T(8,128)(2,1)} fusion(f32[1024,8192]{1,0:T(8,128)} %fusion.53, f32[1024,8192]{1,0:T(8,128)} %fusion.57), kind=kLoop, calls=%fused_computation.34 | loop fusion | flops 50331648 | bytes 83886080
  208.3 29.7 %all-gather.34.cloned.1.call-done = bf16[1,8192,512]{2,1,0:T(8,128)(2,1)} async-done(((bf16[1,512,512]{2,1,0:T(8,128)(2,1)}), bf16[1,8192,512]{2,1,0:T(8,128)(2,1)}) %all-gather.34.cloned.1.call-update) | async-done | bytes 8388624 | tf_op jit(solution)/vmap(jvp())/squeeze | solution.py:27
  238.0 14.9 fusion.67
  253.0 59.8 %all-gather.36.cloned.1.call-done = bf16[1,512,8192]{2,1,0:T(8,128)(2,1)} async-done(((bf16[1,32,8192]{2,1,0:T(8,128)(2,1)}), bf16[1,512,8192]{2,1,0:T(8,128)(2,1)}) %all-gather.36.cloned.1.call-update) | async-done | bytes 8388624 | tf_op jit(solution)/vmap(jvp())/squeeze | solution.py:27
  312.8 19.0 %fusion.47 = f32[1024,8192]{1,0:T(8,128)} fusion(bf16[1,512,8192]{2,1,0:T(8,128)(2,1)} %all-gather.36.cloned.1.call-done, bf16[1,1,1024,512]{2,3,1,0:T(8,128)(2,1)S(1)} %get-tuple-element.15, f32[1024]{0:T(1024)S(1)} %bitcast.320), kind=kOutput, calls=%fused_computation.55 | convolution fusion | flops 8591507456 | bytes 42995712 | tf_op jit(solution)/vmap(jvp())/dot_general | solution.py:20
  331.8 56.4 %all-gather.40.cloned.1.call-done = bf16[1,512,8192]{2,1,0:T(8,128)(2,1)} async-done(((bf16[1,32,8192]{2,1,0:T(8,128)(2,1)}), bf16[1,512,8192]{2,1,0:T(8,128)(2,1)}) %all-gather.40.cloned.1.call-update) | async-done | bytes 8388624 | tf_op jit(solution)/vmap(jvp())/squeeze | solution.py:27
  388.2 18.7 %fusion.41 = f32[1024,8192]{1,0:T(8,128)} fusion(bf16[1,512,8192]{2,1,0:T(8,128)(2,1)} %all-gather.40.cloned.1.call-done, bf16[1,1,1024,512]{2,3,1,0:T(8,128)(2,1)S(1)} %get-tuple-element.15, f32[1024]{0:T(1024)S(1)} %bitcast.321), kind=kOutput, calls=%fused_computation.49 | convolution fusion | flops 8591507456 | bytes 42995712 | tf_op jit(solution)/vmap(jvp())/dot_general | solution.py:21
  406.9 56.1 %all-gather.38.cloned.1.call-done = bf16[1,8192,512]{2,1,0:T(8,128)(2,1)} async-done(((bf16[1,512,512]{2,1,0:T(8,128)(2,1)}), bf16[1,8192,512]{2,1,0:T(8,128)(2,1)}) %all-gather.38.cloned.1.call-update) | async-done | bytes 8388624 | tf_op jit(solution)/vmap(jvp())/squeeze | solution.py:27
  463.0 15.1 convolution_convert_fusion.1
  478.1 27.2 %fusion.4 = bf16[1024,8192]{1,0:T(8,128)(2,1)S(1)} fusion(f32[1024,8192]{1,0:T(8,128)} %fusion.47, f32[1024,8192]{1,0:T(8,128)} %fusion.41, bf16[1024,8192]{1,0:T(8,128)(2,1)} %convolution_convert_fusion.1), kind=kLoop, calls=%fused_computation.10 | loop fusion | flops 100663296 | bytes 100663296
  505.3 5.7 copy-done
  511.1 12.3 fusion.76
  523.4 22.3 %fusion.69 = (f32[1024]{0:T(1024)S(1)}, bf16[1,1,1024,512]{2,3,1,0:T(8,128)(2,1)S(1)}) fusion(bf16[1,1,1024,512]{2,3,1,0:T(8,128)(2,1)S(1)} %get-tuple-element.15, bf16[1024,512]{0,1:T(8,128)(2,1)S(1)} %fusion.76, bf16[1,512,8192]{2,1,0:T(8,128)(2,1)} %all-gather.40.cloned.1.call-done, bf16[1024,8192]{1,0:T(8,128)(2,1)} %convolution_convert_fusion.1, ...), kind=kOutput, calls=%fused_computation.88 | convolution fusion | flops 8643410944 | bytes 61870080 | tf_op jit(solution)/vmap(transpose(jvp()))/dot_general | solution.py:21
  545.7 0.7 fusion.119
  546.4 16.2 convolution_bitcast_fusion
  562.7 0.0 reduce-scatter.27.cloned.1.call-start
  562.8 29.5 %fusion.32 = f32[1,8192,512]{2,1,0:T(8,128)} fusion(f32[1024,8192]{1,0:T(8,128)} %fusion.41, f32[1024,8192]{1,0:T(8,128)} %fusion.47, bf16[1,1024,512]{2,1,0:T(8,128)(2,1)S(1)} %copy-done.12), kind=kOutput, calls=%fused_computation.43 | convolution fusion | flops 8640266240 | bytes 84934656 | tf_op jit(solution)/vmap(transpose(jvp()))/dot_general | solution.py:9
  592.2 0.0 reduce-scatter.23.cloned.1.call-start
  592.3 25.6 %fusion.35 = f32[1,512,8192]{2,1,0:T(8,128)} fusion(bf16[1024,8192]{1,0:T(8,128)(2,1)} %convolution_convert_fusion.1, f32[1024,8192]{1,0:T(8,128)} %fusion.47, bf16[1,1,1024,512]{2,3,1,0:T(8,128)(2,1)S(1)} %get-tuple-element.15, f32[1024]{0:T(1024)S(1)} %bitcast.323), kind=kOutput, calls=%fused_computation.44 | convolution fusion | flops 8641839104 | bytes 68161536 | tf_op jit(solution)/vmap(transpose(jvp()))/dot_general | solution.py:21
  617.9 0.0 reduce-scatter.25.cloned.1.call-start
  618.0 16.1 convolution_convert_fusion
  634.1 27.1 %fusion.7 = bf16[1024,8192]{1,0:T(8,128)(2,1)S(1)} fusion(f32[1024,8192]{1,0:T(8,128)} %fusion.57, f32[1024,8192]{1,0:T(8,128)} %fusion.53, bf16[1024,8192]{1,0:T(8,128)(2,1)} %convolution_convert_fusion), kind=kLoop, calls=%fused_computation.13 | loop fusion | flops 100663296 | bytes 100663296
  661.2 5.7 copy-done.1
  666.9 12.4 fusion.70
  679.3 22.1 %fusion.65 = (f32[1024]{0:T(1024)S(1)}, bf16[1,1,1024,512]{2,3,1,0:T(8,128)(2,1)}) fusion(bf16[1,1024,512]{1,2,0:T(8,128)(2,1)S(1)} %copy-done.6, bf16[1024,512]{0,1:T(8,128)(2,1)S(1)} %fusion.70, bf16[1,512,8192]{2,1,0:T(8,128)(2,1)} %all-gather.32.cloned.1.call-done, bf16[1024,8192]{1,0:T(8,128)(2,1)} %convolution_convert_fusion, f32[1024,8192]{1,0:T(8,128)} %fusion.57), kind=kOutput, calls=%fused_computation.84 | convolution fusion | flops 8643410944 | bytes 61870080 | tf_op jit(solution)/vmap(transpose(jvp()))/dot_general | solution.py:21
  701.4 25.6 %fusion.38 = f32[1,512,8192]{2,1,0:T(8,128)} fusion(bf16[1024,8192]{1,0:T(8,128)(2,1)} %convolution_convert_fusion, f32[1024,8192]{1,0:T(8,128)} %fusion.57, bf16[1,1024,512]{1,2,0:T(8,128)(2,1)S(1)} %copy-done.6, f32[1024]{0:T(1024)S(1)} %bitcast.329), kind=kOutput, calls=%fused_computation.45 | convolution fusion | flops 8641839104 | bytes 68161536 | tf_op jit(solution)/vmap(transpose(jvp()))/dot_general | solution.py:21
  727.0 0.0 reduce-scatter.19.cloned.1.call-start
  727.1 1.1 copy-done.3
  728.2 15.7 convolution_bitcast_fusion.2
  744.0 0.0 reduce-scatter.21.cloned.1.call-start
  744.0 16.0 convolution_bitcast_fusion.1
  760.0 1.2 copy-done.9
  761.2 1.9 fusion.118
  763.1 1.3 copy.2
  764.4 1.3 convert_bitcast_fusion
  765.7 150.2 %reduce-scatter.27.cloned.1.call-done = f32[1,512,512]{2,1,0:T(8,128)} async-done(((f32[1,8192,512]{2,1,0:T(8,128)}), f32[1,512,512]{2,1,0:T(8,128)}) %reduce-scatter.27.cloned.1.call-update) | async-done | bytes 1048592
  915.9 1.3 convert_bitcast_fusion.1
  917.2 1.0 add_bitcast_fusion
  918.3 176.9 %reduce-scatter.23.cloned.1.call-done = f32[1,32,8192]{2,1,0:T(8,128)} async-done(((f32[1,512,8192]{2,1,0:T(8,128)}), f32[1,32,8192]{2,1,0:T(8,128)}) %reduce-scatter.23.cloned.1.call-update) | async-done | bytes 1048592
  1095.2 1.3 convert_bitcast_fusion.3
  1096.5 177.8 %reduce-scatter.25.cloned.1.call-done = f32[1,32,8192]{2,1,0:T(8,128)} async-done(((f32[1,512,8192]{2,1,0:T(8,128)}), f32[1,32,8192]{2,1,0:T(8,128)}) %reduce-scatter.25.cloned.1.call-update) | async-done | bytes 1048592
  1274.3 1.3 convert_bitcast_fusion.2
  1275.6 1.0 add_bitcast_fusion.1
  1276.6 176.9 %reduce-scatter.19.cloned.1.call-done = f32[1,32,8192]{2,1,0:T(8,128)} async-done(((f32[1,512,8192]{2,1,0:T(8,128)}), f32[1,32,8192]{2,1,0:T(8,128)}) %reduce-scatter.19.cloned.1.call-update) | async-done | bytes 1048592
  1453.6 1.3 convert_bitcast_fusion.5
  1454.8 177.8 %reduce-scatter.21.cloned.1.call-done = f32[1,32,8192]{2,1,0:T(8,128)} async-done(((f32[1,512,8192]{2,1,0:T(8,128)}), f32[1,32,8192]{2,1,0:T(8,128)}) %reduce-scatter.21.cloned.1.call-update) | async-done | bytes 1048592
  1632.7 1.3 convert_bitcast_fusion.4
  1634.0 1.0 add_bitcast_fusion.2
  (43 shorter events, 0.5 us)
Async XLA Ops:
  7.2 80.3 %all-gather.30.cloned.1.call-start = ((), (), s32[]{:S(2)}) async-start(), calls=%async_computation.6 | async-start | bytes 8912896 | tf_op jit(solution)/vmap(jvp())/squeeze | solution.py:27
  9.5 153.5 %all-gather.32.cloned.1.call-start = ((), (), s32[]{:S(2)}) async-start(), calls=%async_computation.7 | async-start | bytes 8912896 | tf_op jit(solution)/vmap(jvp())/squeeze | solution.py:27
  11.8 226.2 %all-gather.34.cloned.1.call-start = ((), (), s32[]{:S(2)}) async-start(), calls=%async_computation.8 | async-start | bytes 8912896 | tf_op jit(solution)/vmap(jvp())/squeeze | solution.py:27
  14.2 298.6 %all-gather.36.cloned.1.call-start = ((), (), s32[]{:S(2)}) async-start(), calls=%async_computation.9 | async-start | bytes 8912896 | tf_op jit(solution)/vmap(jvp())/squeeze | solution.py:27
  14.8 373.4 %all-gather.40.cloned.1.call-start = ((), (), s32[]{:S(2)}) async-start(), calls=%async_computation.11 | async-start | bytes 8912896 | tf_op jit(solution)/vmap(jvp())/squeeze | solution.py:27
  15.4 447.6 %all-gather.38.cloned.1.call-start = ((), (), s32[]{:S(2)}) async-start(), calls=%async_computation.10 | async-start | bytes 8912896 | tf_op jit(solution)/vmap(jvp())/squeeze | solution.py:27
  15.9 748.5 %reduce-scatter.29.cloned.1.call-start = ((), (), s32[]{:S(2)}) async-start(), calls=%async_computation.17 | async-start | bytes 17825792
  19.0 219.0 %copy-start.5 = (bf16[1,1024,512]{1,2,0:T(8,128)(2,1)}, bf16[1,1024,512]{1,2,0:T(8,128)(2,1)S(1)}, u32[]{:S(2)}) copy-start(bf16[1,1024,512]{1,2,0:T(8,128)(2,1)S(1)} %copy.1) | copy-start | bytes 3145732
  87.5 75.5 %copy-start.4 = (bf16[1,1024,512]{2,1,0:T(8,128)(2,1)S(1)}, bf16[1,1024,512]{2,1,0:T(8,128)(2,1)}, u32[]{:S(2)}) copy-start(bf16[1,1024,512]{2,1,0:T(8,128)(2,1)} %param.1) | copy-start | bytes 3145732
  252.9 339.4 %copy-start.2 = (bf16[1,1,1024,512]{2,3,1,0:T(8,128)(2,1)}, bf16[1,1,1024,512]{2,3,1,0:T(8,128)(2,1)S(1)}, u32[]{:S(2)}) copy-start(bf16[1,1,1024,512]{2,3,1,0:T(8,128)(2,1)S(1)} %get-tuple-element.15) | copy-start | bytes 3145732
  253.0 339.3 %copy-start.10 = (f32[1,1,1024]{2,1,0:T(1,128)}, f32[1,1,1024]{2,1,0:T(1,128)S(1)}, u32[]{:S(2)}) copy-start(f32[1,1,1024]{2,1,0:T(1,128)S(1)} %rsqrt.23) | copy-start | bytes 12292
  331.8 131.2 %copy-start.12 = (bf16[1,1024,512]{2,1,0:T(8,128)(2,1)S(1)}, bf16[1,1024,512]{2,1,0:T(8,128)(2,1)}, u32[]{:S(2)}) copy-start(bf16[1,1024,512]{2,1,0:T(8,128)(2,1)} %param) | copy-start | bytes 3145732
  505.3 5.7 copy-start
  523.3 22.4 %copy-start.7 = (bf16[1,1024,512]{1,2,0:T(8,128)(2,1)S(1)}, bf16[1,1024,512]{1,2,0:T(8,128)(2,1)}, u32[]{:S(2)}) copy-start(bf16[1,1024,512]{1,2,0:T(8,128)(2,1)} %copy) | copy-start | bytes 3145732
  546.4 71.5 %copy-start.8 = (bf16[1,1,1024,512]{2,3,1,0:T(8,128)(2,1)}, bf16[1,1,1024,512]{2,3,1,0:T(8,128)(2,1)S(1)}, u32[]{:S(2)}) copy-start(bf16[1,1,1024,512]{2,3,1,0:T(8,128)(2,1)S(1)} %fusion.119) | copy-start | bytes 3145732
  562.7 353.2 %reduce-scatter.27.cloned.1.call-start = ((), (), s32[]{:S(2)}) async-start(), calls=%async_computation.16 | async-start | bytes 17825792
  592.2 503.0 %reduce-scatter.23.cloned.1.call-start = ((), (), s32[]{:S(2)}) async-start(), calls=%async_computation.14 | async-start | bytes 17825792
  617.9 656.4 %reduce-scatter.25.cloned.1.call-start = ((), (), s32[]{:S(2)}) async-start(), calls=%async_computation.15 | async-start | bytes 17825792
  661.2 5.7 copy-start.1
  666.9 12.4 copy-start.6
  679.3 22.1 %copy-start.13 = (f32[1024]{0:T(1024)S(1)}, f32[1024]{0:T(1024)}, u32[]{:S(2)}) copy-start(f32[1024]{0:T(1024)} %get-tuple-element.12) | copy-start | bytes 12292
  727.0 1.2 copy-start.3
  727.0 1.2 copy-start.11
  727.0 726.5 %reduce-scatter.19.cloned.1.call-start = ((), (), s32[]{:S(2)}) async-start(), calls=%async_computation.12 | async-start | bytes 17825792
  744.0 888.7 %reduce-scatter.21.cloned.1.call-start = ((), (), s32[]{:S(2)}) async-start(), calls=%async_computation.13 | async-start | bytes 17825792
  760.0 1.2 copy-start.9
Sparse Core Ops, SparseCore 0:
  10.2 77.2 all-gather.29
  90.3 72.7 all-gather.31
  165.2 72.7 all-gather.33
  240.0 72.6 all-gather.35
  315.4 72.6 all-gather.39
  390.2 72.6 all-gather.37
  562.8 173.7 reduce-scatter.28
  740.7 175.1 reduce-scatter.26
  920.0 175.1 reduce-scatter.22
  1099.2 175.1 reduce-scatter.24
  1278.4 175.0 reduce-scatter.18
  1457.5 175.1 reduce-scatter.20
where the time goes:
time: 1650 us; the launch traced here: 1640 us
  waiting for transfers between devices  1190 us (72%)
  matrix products  318 us (19%)
  other arithmetic  97.3 us (6%)
  local copies, waits for them, and re-layouts  25.7 us (2%)
    unnamed x18, waiting for transfers between devices  861 us
    squeeze x6, waiting for transfers between devices, stack(): h = layer(h, {name: w[number] for name, w in weights.items()})  324 us
    dot_general x6, matrix products, layer(): up = jnp.dot(a, w['w_up'], preferred_element_type=jnp.float32)  132 us
    dot_general x6, matrix products, layer(): gate = jnp.dot(a, w['w_gate'], preferred_element_type=jnp.float32)  94.3 us
    dot_general x5, matrix products, matmul(): jnp.dot(a, w, preferred_element_type=jnp.float32).astype(jnp.bfloat16)  91.9 us
    unnamed x3, other arithmetic  81.7 us
  transfers between devices with their start and end apart: 12, of which 11 were waited for; matrix products, arithmetic and copies ran while one was open for 20% of the time, Pallas kernels for 0%

commit v1 on v0

v1 whole, which is shorter than its diff:
```python
import functools

import jax
import jax.numpy as jnp
from jax import lax
from jax.experimental import pallas as pl
from jax.experimental.pallas import tpu as pltpu
from jax.sharding import PartitionSpec as P

MESH = pl.DeviceIdType.MESH
F32, BF16 = jnp.float32, jnp.bfloat16
ROUNDS = 12
ALL = 2 * ROUNDS
T_SLOTS, R_SLOTS, S_SLOTS = 8, 6, 8


def nn(a, b):
    return jnp.dot(a, b, preferred_element_type=F32)


def nt(a, b):
    return lax.dot_general(a, b, (((1,), (1,)), ((), ())), preferred_element_type=F32)


def kernel(tile, x_ref, dy_ref, wgu_ref, wd_ref, dx_ref, og_ref, od_ref, xp_ref, h1_ref,
           W, T, R, A, AT, DY, DYT, ACC, PT, ACT, DG, DU,
           prep_loc, prep_send, prep_rem, ag_send, ag_recv, ax_send, ax_recv,
           rs_send, rs_recv, out_loc, out_send, out_recv, ex_send, ex_recv, loc, credit):
    tok, d = x_ref.shape
    half = wd_ref.shape[3]
    rows = half // 2
    rep, dp = lax.axis_index("rep"), lax.axis_index("dp")
    core, chip = lax.rem(dp, 2), dp // 2
    q = jnp.where(chip < 4, chip, 11 - chip)

    def chip_at(place):
        place = lax.rem(place + 16, 8)
        return jnp.where(place < 4, place, 11 - place)

    ring = tuple((rep, 2 * chip_at(q + step) + core) for step in (1, -1))
    across, mate = (1 - rep, dp), (rep, 2 * chip + 1 - core)

    def remote(src, dst, send, recv, to):
        return pltpu.make_async_remote_copy(
            src_ref=src, dst_ref=dst, send_sem=send, recv_sem=recv, device_id=to, device_id_type=MESH
        )

    barrier = pltpu.get_barrier_semaphore()
    for other in (*ring, across, mate):
        pl.semaphore_signal(barrier, inc=1, device_id=other, device_id_type=MESH)

    mine, theirs = pl.ds(core * tok, tok), pl.ds((1 - core) * tok, tok)
    own_rows = pl.ds(pl.multiple_of(core * rows, rows), rows)
    mate_rows = pl.ds(pl.multiple_of((1 - core) * rows, rows), rows)

    def prep_down(r):
        return pltpu.make_async_copy(wd_ref.at[r // ROUNDS, lax.rem(r, ROUNDS) // 3], W.at[r, chip], prep_loc.at[r])

    def up_index(r):
        return lax.rem(r, ROUNDS) // 3, jnp.maximum(lax.rem(r, 3) - 1, 0)

    def prep_here(r):
        dst = W.at[r, chip, :, own_rows]
        return pltpu.make_async_copy(wgu_ref.at[(r // ROUNDS, core, *up_index(r))], dst, prep_loc.at[r])

    def prep_there(r):
        src, dst = wgu_ref.at[(r // ROUNDS, 1 - core, *up_index(r))], W.at[r, chip, :, own_rows]
        return remote(src, dst, prep_send.at[r], prep_rem.at[r], mate)

    def start_local(r, _):
        @pl.when(lax.rem(r, 3) == 0)
        def _():
            prep_down(r).start()

        @pl.when(lax.rem(r, 3) != 0)
        def _():
            prep_here(r).start()

        return 0

    lax.fori_loop(0, ALL, start_local, 0)
    load_x = pltpu.make_async_copy(x_ref, A.at[mine], loc.at[0])
    load_dy = pltpu.make_async_copy(dy_ref, DY.at[mine], loc.at[1])
    load_x.start()
    load_dy.start()
    pl.semaphore_wait(barrier, 4)

    def start_mate(r, _):
        @pl.when(lax.rem(r, 3) != 0)
        def _():
            prep_there(r).start()

        return 0

    send_x = remote(x_ref, A.at[mine], ex_send.at[0], ex_recv.at[0], mate)
    send_xp = remote(x_ref, xp_ref, ex_send.at[1], ex_recv.at[1], mate)
    send_dy = remote(dy_ref, DY.at[mine], ex_send.at[2], ex_recv.at[2], mate)
    lax.fori_loop(0, 3, start_mate, 0)
    send_x.start()
    lax.fori_loop(3, ALL, start_mate, 0)
    send_xp.start()
    send_dy.start()

    def wait_prep(r):
        @pl.when(lax.rem(r, 3) == 0)
        def _():
            prep_down(r).wait()

        @pl.when(lax.rem(r, 3) != 0)
        def _():
            prep_here(r).wait()
            prep_there(r).wait_recv()

    def kind(r):
        return lax.rem(r, 3)

    def hops(r, way):
        return 4 - lax.rem(r + way + 8, 2)

    def gathers(r):
        return (kind(r) == 2) | (kind(r) == rep)

    def ag_copy(r, way, h):
        piece = W.at[r, chip_at(q - h if way == 0 else q + h)]
        return remote(piece, piece, ag_send.at[lax.rem(r, S_SLOTS), way, h], ag_recv.at[r, way, h], ring[way])

    def ag_retire(r):
        for way in (0, 1):
            for h in range(4):
                @pl.when(gathers(r) & (h < hops(r, way)))
                def _():
                    ag_copy(r, way, h).wait_send()

    def ag_event(n, h):
        r = n - h
        ok = (r >= 0) & (r < ALL)

        @pl.when(ok & (h == 0))
        def _():
            wait_prep(r)

            @pl.when(r >= S_SLOTS)
            def _():
                ag_retire(r - S_SLOTS)

        @pl.when(ok & gathers(jnp.maximum(r, 0)))
        def _():
            for way in (0, 1):
                @pl.when(h == 0)
                def _():
                    ag_copy(r, way, 0).start()

                @pl.when((h > 0) & (h <= hops(r, way)))
                def _():
                    piece = W.at[r, chip_at(q - h if way == 0 else q + h)]
                    remote(piece, piece, ag_send.at[0, way, 0], ag_recv.at[r, way, h - 1], ring[way]).wait_recv()

                    @pl.when(h < hops(r, way))
                    def _():
                        ag_copy(r, way, h).start()

                    @pl.when(kind(r) != 2)
                    def _():
                        remote(piece, piece, ax_send.at[r], ax_recv.at[r], across).start()

    def ag_ready(r):
        @pl.when(jnp.logical_not(gathers(r)))
        def _():
            seven = W.at[r, pl.ds(0, 7)]
            remote(seven, seven, ax_send.at[r], ax_recv.at[r], across).wait_recv()

    def ag_events(lo, hi):
        def body(e, _):
            ag_event(e // 5, 4 - lax.rem(e, 5))
            return 0

        lax.fori_loop(lo, hi, body, 0)

    def rs_copy(n, way, h):
        slot = lax.rem(n, T_SLOTS)
        step = hops(n, way) - h
        return remote(
            T.at[slot, chip_at(q + step if way == 0 else q - step)],
            R.at[lax.rem(n, R_SLOTS), 4 * way + h],
            rs_send.at[slot, way, h],
            rs_recv.at[lax.rem(n, R_SLOTS), way, h],
            ring[way],
        )

    def out_down(n):
        slot = lax.rem(n, T_SLOTS)
        return pltpu.make_async_copy(
            T.at[slot, chip], od_ref.at[1 - n // ROUNDS, lax.rem(n, ROUNDS) // 3], out_loc.at[slot]
        )

    def out_up(n):
        return og_ref.at[1 - n // ROUNDS, core, lax.rem(n, ROUNDS) // 3, jnp.minimum(lax.rem(n, 3), 1)]

    def out_here(n):
        slot = lax.rem(n, T_SLOTS)
        return pltpu.make_async_copy(T.at[slot, chip, :, own_rows], out_up(n), out_loc.at[slot])

    def out_there(n):
        slot = lax.rem(n, T_SLOTS)
        return remote(T.at[slot, chip, :, mate_rows], out_up(n), out_send.at[slot], out_recv.at[n], mate)

    def rs_retire(n):
        for way in (0, 1):
            for h in range(4):
                @pl.when(h < hops(n, way))
                def _():
                    rs_copy(n, way, h).wait_send()

        @pl.when(kind(n) == 2)
        def _():
            out_down(n).wait()

        @pl.when(kind(n) != 2)
        def _():
            out_here(n).wait()
            out_there(n).wait_send()

    def rs_event(n0, h):
        n = n0 - h
        ok = (n >= 0) & (n < ALL)

        @pl.when(ok)
        def _():
            slot, rslot = lax.rem(n, T_SLOTS), lax.rem(n, R_SLOTS)
            for way in (0, 1):
                @pl.when(h == 0)
                def _():
                    @pl.when(n >= R_SLOTS)
                    def _():
                        pl.semaphore_wait(credit.at[way], 1)

                    rs_copy(n, way, 0).start()

                @pl.when((h > 0) & (h <= hops(n, way)))
                def _():
                    rs_copy(n, way, h - 1).wait_recv()

                    @pl.when(h < hops(n, way))
                    def _():
                        step = hops(n, way) - h
                        own = chip_at(q + step if way == 0 else q - step)
                        total = T[slot, own].astype(F32) + R[rslot, 4 * way + h - 1].astype(F32)
                        T[slot, own] = total.astype(BF16)
                        rs_copy(n, way, h).start()

            @pl.when(h == 4)
            def _():
                total = T[slot, chip].astype(F32) + R[rslot, hops(n, 0) - 1].astype(F32)
                total = total + R[rslot, 4 + hops(n, 1) - 1].astype(F32)
                T[slot, chip] = total.astype(BF16)

                @pl.when(kind(n) == 2)
                def _():
                    out_down(n).start()

                @pl.when(kind(n) != 2)
                def _():
                    out_here(n).start()
                    out_there(n).start()

                @pl.when(n < ALL - R_SLOTS)
                def _():
                    for way in (0, 1):
                        pl.semaphore_signal(credit.at[way], inc=1, device_id=ring[1 - way], device_id_type=MESH)

    def rs_events(lo, hi):
        def body(e, _):
            rs_event(e // 5, 4 - lax.rem(e, 5))
            return 0

        lax.fori_loop(lo, hi, body, 0)

    block = min(256, tok)
    blocks = 2 * tok // block

    def part(t, size=block):
        return pl.ds(pl.multiple_of(t * size, size), size)

    def normed(h):
        wide = h.astype(F32)
        return (wide * lax.rsqrt(jnp.mean(wide * wide, -1, keepdims=True) + 1e-6)).astype(BF16)

    def norm_all(flip):
        def body(t, _):
            a = normed(A[part(t), :])
            A[part(t), :] = a
            if flip:
                AT[:, part(t)] = a.T
            return 0

        lax.fori_loop(0, blocks, body, 0)

    def flip_dy():
        def body(t, _):
            DYT[:, part(t)] = DY[part(t), :].T
            return 0

        lax.fori_loop(0, blocks, body, 0)

    def clear():
        def body(t, _):
            ACC[part(t), :] = jnp.zeros((block, d), F32)
            return 0

        lax.fori_loop(0, blocks, body, 0)

    def own_block(t):
        return pl.ds(pl.multiple_of(core * tok + t * block, block), block)

    def forward(j):
        i, hh = j // 2, lax.rem(j, 2)
        r = 3 * i + 1 + hh

        def body(t, _):
            at = A[part(t, tile), :]
            gate = nn(at, W[r, :, 0].reshape(d, -1))
            up = nn(at, W[r, :, 1].reshape(d, -1))
            act = (gate * (0.5 * jnp.tanh(0.5 * gate) + 0.5) * up).astype(BF16)
            ACC[part(t, tile), :] += nn(act, W[3 * i, pl.ds(4 * hh, 4)].reshape(-1, d))
            return 0

        lax.fori_loop(0, 2 * tok // tile, body, 0)

    def first(n, _):
        @pl.when(n == 1)
        def _():
            load_x.wait()
            send_x.wait_recv()
            norm_all(False)
            clear()

        @pl.when(n == 3)
        def _():
            load_dy.wait()
            send_dy.wait_recv()
            flip_dy()

        pair = (n - 4) // 3

        @pl.when((n >= 4) & (lax.rem(n, 3) == 0))
        def _():
            ag_ready(3 * pair)
            ag_ready(3 * pair + 1)
            forward(2 * pair)

        ag_events(5 * n, 5 * n + 5)

        @pl.when((n >= 4) & (lax.rem(n, 3) == 0))
        def _():
            ag_ready(3 * pair + 2)
            forward(2 * pair + 1)

        return 0

    lax.fori_loop(0, 16, first, 0)

    swap = remote(ACC.at[theirs], PT, ex_send.at[3], ex_recv.at[3], mate)
    swap.start()
    fetch = pltpu.make_async_copy(x_ref, DG.at[pl.ds(0, tok)], loc.at[2])
    fetch.start()
    ag_events(80, 85)
    fetch.wait()
    swap.wait()

    def residual(t, _):
        mlp = (ACC[own_block(t), :] + PT[part(t), :]).astype(BF16)
        h = (DG[part(t), :].astype(F32) + mlp.astype(F32)).astype(BF16)
        ACT[part(t), :] = h
        A[own_block(t), :] = h
        return 0

    lax.fori_loop(0, tok // block, residual, 0)
    h1 = ACT.at[pl.ds(0, tok)]
    send_h = remote(h1, A.at[mine], ex_send.at[4], ex_recv.at[4], mate)
    keep_h = pltpu.make_async_copy(h1, h1_ref, loc.at[3])
    send_h.start()
    keep_h.start()
    clear()
    ag_events(85, 90)
    send_h.wait()
    keep_h.wait()
    norm_all(True)

    def norm_back(h_ref, t):
        by_a = (ACC[own_block(t), :] + PT[part(t), :]).astype(BF16).astype(F32)
        wide = h_ref[part(t), :].astype(F32)
        scale = lax.rsqrt(jnp.mean(wide * wide, -1, keepdims=True) + 1e-6)
        along = jnp.mean(by_a * wide, -1, keepdims=True)
        by_h = (by_a * scale - wide * (scale * scale * scale * along)).astype(BF16)
        return (DY[own_block(t), :].astype(F32) + by_h.astype(F32)).astype(BF16)

    def chunk(c, _):
        l = 1 - c // 8
        j = lax.rem(c, 8)
        i, hh = j // 2, lax.rem(j, 2)
        pair = c // 2
        base = ROUNDS * l + 3 * i
        up_slot, down_slot = lax.rem(3 * pair + hh, T_SLOTS), lax.rem(3 * pair + 2, T_SLOTS)

        def serve(slot):
            ag_lo, ag_hi = 90 + 10 * c + (10 * slot) // 8, 90 + 10 * c + (10 * slot + 10) // 8
            ag_events(jnp.minimum(ag_lo, 140), jnp.minimum(ag_hi, 140))
            odd = lax.rem(c, 2) == 1
            count = jnp.where(odd | (c == 8), 5, 10)
            start = jnp.where(odd, 15 * pair, 15 * pair - count)
            lo, hi = start + (count * slot) // 8, start + (count * slot + count) // 8
            rs_events(jnp.maximum(lo, 0), jnp.maximum(hi, 0))

        @pl.when(c == 8)
        def _():
            swap = remote(ACC.at[theirs], PT, ex_send.at[5], ex_recv.at[5], mate)
            swap.start()
            fetch = pltpu.make_async_copy(h1_ref, DG.at[pl.ds(0, tok)], loc.at[4])
            fetch.start()
            rs_events(50, 53)
            fetch.wait()
            swap.wait()

            def body(t, _):
                dh = norm_back(DG, t)
                DY[own_block(t), :] = dh
                ACT[part(t), :] = dh
                return 0

            lax.fori_loop(0, tok // block, body, 0)
            send = remote(ACT.at[pl.ds(0, tok)], DY.at[mine], ex_send.at[6], ex_recv.at[6], mate)
            send.start()
            again = pltpu.make_async_copy(x_ref, A.at[mine], loc.at[5])
            again.start()
            send_xp.wait_recv()
            other = pltpu.make_async_copy(xp_ref, A.at[theirs], loc.at[6])
            other.start()
            clear()
            rs_events(53, 55)
            again.wait()
            other.wait()
            norm_all(True)
            send.wait()
            flip_dy()

        @pl.when(l == 1)
        def _():
            @pl.when(hh == 0)
            def _():
                ag_ready(base)

            ag_ready(base + 1 + hh)

        def tokens(t, _):
            s = part(t, tile)
            at = A[s, :]
            wg, wu = W[base + 1 + hh, :, 0].reshape(d, -1), W[base + 1 + hh, :, 1].reshape(d, -1)
            gate, up = nn(at, wg), nn(at, wu)
            by_act = nt(DY[s, :], W[base, pl.ds(4 * hh, 4)].reshape(-1, d)).astype(BF16).astype(F32)
            sig = 0.5 * jnp.tanh(0.5 * gate) + 0.5
            silu = gate * sig
            ACT[s, :] = (silu * up).astype(BF16)
            dup = (by_act * silu).astype(BF16)
            dgate = (by_act * up * (sig + silu * (1.0 - sig))).astype(BF16)
            DG[s, :] = dgate
            DU[s, :] = dup
            ACC[s, :] += nt(dgate, wg) + nt(dup, wu)
            serve(t * (4 * tile) // (2 * tok))
            return 0

        lax.fori_loop(0, 2 * tok // tile, tokens, 0)

        for back, when in ((0, 0), (1, 1), (2, 0)):
            n = 3 * pair + back - T_SLOTS

            @pl.when((hh == when) & (n >= 0))
            def _():
                rs_retire(n)

        def grads_up(p, _):
            s = pl.ds(pl.multiple_of(p * (d // 2), d // 2), d // 2)
            T[up_slot, pl.ds(4 * p, 4), 0] = nn(AT[s, :], DG[...]).astype(BF16).reshape(4, half, -1)
            T[up_slot, pl.ds(4 * p, 4), 1] = nn(AT[s, :], DU[...]).astype(BF16).reshape(4, half, -1)
            serve(4 + p)
            return 0

        lax.fori_loop(0, 2, grads_up, 0)

        for p in range(2):
            s = slice(p * (d // 2), (p + 1) * (d // 2))
            g = nn(DYT[s, :], ACT[...]).T.astype(BF16)
            T[down_slot, pl.ds(4 * hh, 4), :, :, s] = g.reshape(4, 2, half, d // 2)
            serve(6 + p)

        return 0

    lax.fori_loop(0, 16, chunk, 0)

    swap = remote(ACC.at[theirs], PT, ex_send.at[7], ex_recv.at[7], mate)
    swap.start()
    fetch = pltpu.make_async_copy(x_ref, DG.at[pl.ds(0, tok)], loc.at[7])
    fetch.start()
    rs_events(110, 115)
    fetch.wait()
    swap.wait()

    def last(t, _):
        ACT[part(t), :] = norm_back(DG, t)
        return 0

    lax.fori_loop(0, tok // block, last, 0)
    put = pltpu.make_async_copy(ACT.at[pl.ds(0, tok)], dx_ref, loc.at[8])
    put.start()
    rs_events(115, 140)

    put.wait()
    for copy in (send_x, send_xp, send_dy):
        copy.wait_send()

    def sent(r, _):
        @pl.when(lax.rem(r, 3) != 0)
        def _():
            prep_there(r).wait_send()

        @pl.when((kind(r) != 2) & (kind(r) == rep))
        def _():
            seven = W.at[r, pl.ds(0, 7)]
            remote(seven, seven, ax_send.at[r], ax_recv.at[r], across).wait_send()

        @pl.when(r >= ALL - S_SLOTS)
        def _():
            ag_retire(r)

        @pl.when(r >= ALL - T_SLOTS)
        def _():
            rs_retire(r)

        @pl.when(kind(r) != 2)
        def _():
            out_there(r).wait_recv()

        return 0

    lax.fori_loop(0, ALL, sent, 0)


def of_a_device(x, dy, w_gate, w_up, w_down):
    _, tok, d = x.shape
    layers, rows, ff = w_gate.shape
    half = 2 * rows
    strip = ff // 64
    wgu = jnp.stack((w_gate, w_up)).reshape(2, layers, rows, 2, 4, 2, 4, strip)
    wgu = wgu.transpose(1, 5, 6, 3, 0, 2, 4, 7).reshape(layers, 2, 4, 2, 2, rows, 4 * strip)
    wd = w_down.reshape(layers, 4, 2, half, d)
    hbm = pl.BlockSpec(memory_space=pltpu.HBM)
    tile = tok // 2
    piece = (2, half, d)
    both = 2 * tok
    dx, og, od, _, _ = pl.pallas_call(
        functools.partial(kernel, tile),
        out_shape=(
            jax.ShapeDtypeStruct((tok, d), BF16),
            jax.ShapeDtypeStruct(wgu.shape, BF16),
            jax.ShapeDtypeStruct(wd.shape, BF16),
            jax.ShapeDtypeStruct((tok, d), BF16),
            jax.ShapeDtypeStruct((tok, d), BF16),
        ),
        in_specs=[hbm] * 4,
        out_specs=[hbm] * 5,
        scratch_shapes=[
            pltpu.VMEM((ALL, 8, *piece), BF16),
            pltpu.VMEM((T_SLOTS, 8, *piece), BF16),
            pltpu.VMEM((R_SLOTS, 8, *piece), BF16),
            pltpu.VMEM((both, d), BF16),
            pltpu.VMEM((d, both), BF16),
            pltpu.VMEM((both, d), BF16),
            pltpu.VMEM((d, both), BF16),
            pltpu.VMEM((both, d), F32),
            pltpu.VMEM((tok, d), F32),
            pltpu.VMEM((both, 4 * strip), BF16),
            pltpu.VMEM((both, 4 * strip), BF16),
            pltpu.VMEM((both, 4 * strip), BF16),
            pltpu.SemaphoreType.DMA((ALL,)),
            pltpu.SemaphoreType.DMA((ALL,)),
            pltpu.SemaphoreType.DMA((ALL,)),
            pltpu.SemaphoreType.DMA((S_SLOTS, 2, 4)),
            pltpu.SemaphoreType.DMA((ALL, 2, 4)),
            pltpu.SemaphoreType.DMA((ALL,)),
            pltpu.SemaphoreType.DMA((ALL,)),
            pltpu.SemaphoreType.DMA((T_SLOTS, 2, 4)),
            pltpu.SemaphoreType.DMA((R_SLOTS, 2, 4)),
            pltpu.SemaphoreType.DMA((T_SLOTS,)),
            pltpu.SemaphoreType.DMA((T_SLOTS,)),
            pltpu.SemaphoreType.DMA((ALL,)),
            pltpu.SemaphoreType.DMA((8,)),
            pltpu.SemaphoreType.DMA((8,)),
            pltpu.SemaphoreType.DMA((9,)),
            pltpu.SemaphoreType.REGULAR((2,)),
        ],
        compiler_params=pltpu.CompilerParams(
            collective_id=0, has_side_effects=True, vmem_limit_bytes=67043328
        ),
    )(x[0], dy[0], wgu, wd)
    og = og.reshape(layers, 2, 4, 2, 2, rows, 4, strip)
    og = og.transpose(4, 0, 5, 3, 6, 1, 2, 7).reshape(2, layers, rows, ff)
    return dx[None], og[0], og[1], od.reshape(layers, 4 * 2 * half, d)


def solution(mesh):
    by_seq, by_row = P(("rep", "dp"), None, None), P(None, "dp", None)
    out = P("rep", "dp", None)
    return jax.shard_map(
        of_a_device,
        mesh=mesh,
        in_specs=(by_seq, by_seq, by_row, by_row, by_row),
        out_specs=(by_seq, out, out, out),
        check_vma=False,
    )
```

time: 1650 us -> 458 us (0.28)
  waiting for transfers between devices: 1190 us -> 0 us
  Pallas kernels: 0 us -> 436 us
  matrix products: 318 us -> 0 us
  other arithmetic: 97.3 us -> 1.36 us
    unnamed x18 -> x0, waiting for transfers between devices: 861 us -> none
    pallas_call x0 -> x1, Pallas kernels: none -> 436 us  [of_a_device(): pl.pallas_call(functools.partial(kernel, tile), out_shape=(jax.ShapeDtype...]
    squeeze x6 -> x0, waiting for transfers between devices: 324 us -> none  [stack(): h = layer(h, {name: w[number] for name, w in weights.items()})]
    dot_general x17 -> x0, matrix products: 318 us -> none  [the longest x6 132 us: layer(): up = jnp.dot(a, w['w_up'], preferred_element_type=jnp.float32)]
    unnamed x3 -> x0, other arithmetic: 81.7 us -> none
    unnamed x31 -> x8, local copies, waits for them, and re-layouts: 18.9 us -> 1.95 us
  transfers between devices with their start and end apart: 12 -> 0, of which waited for: 11 -> 0; matrix products, arithmetic and copies ran while one was open for 20% -> 0% of each run, Pallas kernels for 0% -> 0%
where the time goes in v1:
time: 458 us; the launch traced here: 456 us
  Pallas kernels  436 us (95%)
  local copies, waits for them, and re-layouts  17.5 us (4%)
    pallas_call x1, Pallas kernels, of_a_device(): pl.pallas_call(functools.partial(kernel, tile), out_shape=(jax.ShapeDtype...  436 us

profile of v1, /device:TPU:0, one launch (start us, length us, event | category | flops | bytes accessed | tf_op | source)
XLA Modules:
  0.0 455.6 jit_solution(296617079230072625)
XLA Ops:
  0.6 0.0 copy-start
  0.6 1.9 stack.9
  2.5 0.5 copy.9
  3.1 0.0 copy-done
  3.1 0.8 stack.10
  3.9 0.5 copy.10
  4.4 1.4 maximum_bitcast_fusion
  5.8 2.2 reshape.30.wgu_ref
  8.0 436.0 %shard_map.84 = (bf16[1024,512]{1,0:T(8,128)(2,1)}, bf16[2,2,4,2,2,32,512]{6,5,4,3,2,1,0:T(8,128)(2,1)}, bf16[2,4,2,64,512]{4,3,2,1,0:T(8,128)(2,1)}, bf16[1024,512]{1,0:T(8,128)(2,1)}, bf16[1024,512]{1,0:T(8,128)(2,1)}) custom-call(bf16[1024,512]{1,0:T(8,128)(2,1)} %bitcast.11, bf16[1024,512]{1,0:T(8,128)(2,1)} %bitcast.12, ...), custom_call_target="tpu_custom_call" | custom-call | tf_op jit(solution)/shard_map/pallas_call | solution.py:559
  444.0 2.6 reshape.32
  446.5 1.1 fusion
  447.7 1.4 copy.12
  449.0 1.6 squeeze.15
  450.6 0.0 copy-start.2
  450.6 1.4 copy.11
  452.0 0.0 copy-start.1
  452.0 1.6 squeeze.14
  453.6 0.0 copy-done.2
  453.6 1.0 copy.15
  454.6 0.0 copy-done.1
  454.6 1.0 copy.16
Async XLA Ops:
  0.6 2.4 copy-start
  450.6 3.0 copy-start.2
  452.0 2.6 copy-start.1

commit v2 on v1

v2 whole, which is shorter than its diff:
```python
import functools

import jax
import jax.numpy as jnp
from jax import lax
from jax.experimental import pallas as pl
from jax.experimental.pallas import tpu as pltpu
from jax.sharding import PartitionSpec as P

MESH = pl.DeviceIdType.MESH
F32, BF16 = jnp.float32, jnp.bfloat16
ROUNDS = 12
ALL = 2 * ROUNDS
T_SLOTS, R_SLOTS, S_SLOTS = 8, 6, 8
BETWEEN = 48, 54


def events_by(c):
    return jnp.where(c <= 8, jnp.maximum((13 * c - 8) // 2, 0), (15 * c - 11) // 2)


def nn(a, b):
    return jnp.dot(a, b, preferred_element_type=F32)


def nt(a, b):
    return lax.dot_general(a, b, (((1,), (1,)), ((), ())), preferred_element_type=F32)


def kernel(tile, x_ref, dy_ref, wg_ref, wu_ref, wd_ref, dx_ref, og_ref, od_ref, xp_ref, h1_ref,
           W, R, A, AT, DY, DYT, ACC, PT, ACT, DG, DU,
           prep_loc, prep_up, prep_send, prep_rem, ag_send, ag_recv, ax_send, ax_recv,
           rs_send, rs_recv, out_loc, out_send, out_recv, ex_send, ex_recv, sw_send, sw_recv, loc, credit):
    tok, d = x_ref.shape
    half = wd_ref.shape[3]
    rows = half // 2
    strip = wg_ref.shape[2] // 64
    assert d == 4 * strip and half == strip // 2
    rep, dp = lax.axis_index("rep"), lax.axis_index("dp")
    core, chip = lax.rem(dp, 2), dp // 2
    q = jnp.where(chip < 4, chip, 11 - chip)

    def chip_at(place):
        place = lax.rem(place + 16, 8)
        return jnp.where(place < 4, place, 11 - place)

    ring = tuple((rep, 2 * chip_at(q + step) + core) for step in (1, -1))
    across, mate = (1 - rep, dp), (rep, 2 * chip + 1 - core)

    def remote(src, dst, send, recv, to):
        return pltpu.make_async_remote_copy(
            src_ref=src, dst_ref=dst, send_sem=send, recv_sem=recv, device_id=to, device_id_type=MESH
        )

    barrier = pltpu.get_barrier_semaphore()
    for other in (*ring, across, mate):
        pl.semaphore_signal(barrier, inc=1, device_id=other, device_id_type=MESH)

    mine, theirs = pl.ds(core * tok, tok), pl.ds((1 - core) * tok, tok)
    own_rows = pl.ds(pl.multiple_of(core * rows, rows), rows)
    mate_rows = pl.ds(pl.multiple_of((1 - core) * rows, rows), rows)

    def kind(r):
        return lax.rem(r, 3)

    def prep_down(r):
        src = wd_ref.at[r // ROUNDS, lax.rem(r, ROUNDS) // 3]
        return pltpu.make_async_copy(src, W.at[r, chip], prep_loc.at[r // 3])

    def staged(l, g, b, columns=slice(None)):
        spot = 16 * g + b
        return 8 * l + spot // 4, lax.rem(spot // 2, 2), pl.ds(pl.multiple_of(rows * lax.rem(spot, 2), rows), rows), columns

    def load_up(l):
        def body(b, _):
            for g, ref in enumerate((wg_ref, wu_ref)):
                src = ref.at[l, :, pl.ds(pl.multiple_of(d * b, d), d)]
                pltpu.make_async_copy(src, R.at[staged(l, g, b)], prep_up.at[l]).start()
            return 0

        lax.fori_loop(0, 16, body, 0)

    def loaded_up(l):
        eight = R.at[pl.ds(8 * l, 8)]
        pltpu.make_async_copy(eight, eight, prep_up.at[l]).wait()

    def up_number(r):
        return 2 * (r // 3) + kind(r) - 1

    def mate_part(r, g):
        return pl.ds(pl.multiple_of((2 * up_number(r) + g) * rows, rows), rows)

    def prep_start(r):
        l, i, hh = r // ROUNDS, lax.rem(r, ROUNDS) // 3, kind(r) - 1
        columns = pl.ds(pl.multiple_of(strip * i, strip), strip)
        for g in range(2):
            for s in range(4):
                place = slice(strip * s, strip * (s + 1))
                b = 2 * (4 * hh + s)
                W[r, chip, g, own_rows, place] = R[staged(l, g, b + core, columns)]
                DG[mate_part(r, g), place] = R[staged(l, g, b + 1 - core, columns)]
            dst = W.at[r, chip, g, own_rows]
            remote(DG.at[mate_part(r, g)], dst, prep_send, prep_rem.at[up_number(r)], mate).start()

    def prep_there(r):
        part = W.at[r, chip, :, own_rows]
        return remote(part, part, prep_send, prep_rem.at[up_number(r)], mate)

    def prep_first(r, _):
        prep_down(3 * r).start()
        return 0

    load_up(0)
    lax.fori_loop(0, ALL // 3, prep_first, 0)
    load_up(1)

    def prep_all(lo, hi):
        def body(r, _):
            @pl.when(kind(r) != 0)
            def _():
                prep_start(r)

            return 0

        lax.fori_loop(lo, hi, body, 0)

    load_x = pltpu.make_async_copy(x_ref, A.at[mine], loc.at[0])
    load_dy = pltpu.make_async_copy(dy_ref, DY.at[mine], loc.at[1])
    load_x.start()
    load_dy.start()
    pl.semaphore_wait(barrier, 4)

    send_x = remote(x_ref, A.at[mine], ex_send.at[0], ex_recv.at[0], mate)
    send_xp = remote(x_ref, xp_ref, ex_send.at[1], ex_recv.at[1], mate)
    send_dy = remote(dy_ref, DY.at[mine], ex_send.at[2], ex_recv.at[2], mate)
    loaded_up(0)
    prep_all(0, 3)
    send_x.start()
    send_xp.start()
    send_dy.start()

    def wait_prep(r):
        @pl.when(lax.rem(r, 3) == 0)
        def _():
            prep_down(r).wait()

        @pl.when(lax.rem(r, 3) != 0)
        def _():
            prep_there(r).wait_recv()

    def hops(r, way):
        return 4 - lax.rem(r + way + 8, 2)

    def shared(r):
        return (r >= ROUNDS) | (kind(r) != 2)

    def gathers(r):
        first = (kind(r) == 2) | (kind(r) == rep)
        return jnp.where(r < ROUNDS, first, lax.rem(r, 2) == rep)

    def ag_copy(r, way, h):
        piece = W.at[r, chip_at(q - h if way == 0 else q + h)]
        return remote(piece, piece, ag_send.at[lax.rem(r, S_SLOTS), way], ag_recv.at[lax.rem(r, S_SLOTS), way, h], ring[way])

    def ag_retire(r):
        for way in (0, 1):
            for count in (3, 4):
                @pl.when(gathers(r) & (hops(r, way) == count))
                def _():
                    sent = W.at[r, pl.ds(0, count)]
                    remote(sent, sent, ag_send.at[lax.rem(r, S_SLOTS), way], ag_recv.at[0, way, 0], ring[way]).wait_send()

    def ag_event(n, h):
        r = n - h
        ok = (r >= 0) & (r < ALL)

        @pl.when(ok & (h == 0))
        def _():
            wait_prep(r)

            @pl.when(r >= S_SLOTS)
            def _():
                ag_retire(r - S_SLOTS)

        @pl.when(ok & gathers(jnp.maximum(r, 0)))
        def _():
            for way in (0, 1):
                @pl.when(h == 0)
                def _():
                    ag_copy(r, way, 0).start()

                @pl.when((h > 0) & (h <= hops(r, way)))
                def _():
                    piece = W.at[r, chip_at(q - h if way == 0 else q + h)]
                    ag_copy(r, way, h - 1).wait_recv()

                    @pl.when(h < hops(r, way))
                    def _():
                        ag_copy(r, way, h).start()

                    @pl.when(shared(r))
                    def _():
                        remote(piece, piece, ax_send.at[r // ROUNDS], ax_recv.at[r], across).start()

    def ag_ready(r):
        @pl.when(jnp.logical_not(gathers(r)))
        def _():
            seven = W.at[r, pl.ds(0, 7)]
            remote(seven, seven, ax_send.at[0], ax_recv.at[r], across).wait_recv()

    def across_sent(l):
        some = W.at[pl.ds(0, 7), pl.ds(0, 4)] if l == 0 else W.at[pl.ds(0, 7), pl.ds(0, 6)]
        remote(some, some, ax_send.at[l], ax_recv.at[0], across).wait_send()

    def ag_events(lo, hi):
        def body(e, _):
            ag_event(e // 5, 4 - lax.rem(e, 5))
            return 0

        lax.fori_loop(lo, hi, body, 0)

    def term(n):
        return jnp.where(n < ROUNDS, ALL + lax.rem(n, T_SLOTS), n)

    def own_sem(n):
        return lax.rem(n, T_SLOTS)

    def came(n, way, h):
        return 7 * lax.rem(n, R_SLOTS) + (h if way == 0 else hops(n, 0) + h)

    def rs_copy(n, way, h):
        slot = own_sem(n)
        step = hops(n, way) - h
        return remote(
            W.at[term(n), chip_at(q + step if way == 0 else q - step)],
            R.at[came(n, way, h)],
            rs_send.at[slot, way],
            rs_recv.at[lax.rem(n, R_SLOTS), way, h],
            ring[way],
        )

    def out_down(n):
        return pltpu.make_async_copy(
            W.at[term(n), chip], od_ref.at[1 - n // ROUNDS, lax.rem(n, ROUNDS) // 3], out_loc.at[own_sem(n)]
        )

    def out_up(n):
        return og_ref.at[1 - n // ROUNDS, core, lax.rem(n, ROUNDS) // 3, jnp.minimum(kind(n), 1)]

    def out_here(n):
        return pltpu.make_async_copy(W.at[term(n), chip, :, own_rows], out_up(n), out_loc.at[own_sem(n)])

    def out_there(n):
        part = W.at[term(n), chip, :, mate_rows]
        number = 2 * (n // 3) + jnp.minimum(kind(n), 1)
        return remote(part, out_up(n), out_send.at[own_sem(n)], out_recv.at[number], mate)

    def rs_retire(n):
        for way in (0, 1):
            for count in (3, 4):
                @pl.when(hops(n, way) == count)
                def _():
                    sent = W.at[term(n), pl.ds(0, count)]
                    remote(sent, sent, rs_send.at[own_sem(n), way], rs_recv.at[0, way, 0], ring[way]).wait_send()

        @pl.when(kind(n) == 2)
        def _():
            out_down(n).wait()

        @pl.when(kind(n) != 2)
        def _():
            out_here(n).wait()
            out_there(n).wait_send()

    def rs_event(n0, h):
        n = n0 - h
        ok = (n >= 0) & (n < ALL)

        @pl.when(ok)
        def _():
            slot = term(n)
            for way in (0, 1):
                @pl.when(h == 0)
                def _():
                    @pl.when(n >= R_SLOTS)
                    def _():
                        pl.semaphore_wait(credit.at[way], 1)

                    rs_copy(n, way, 0).start()

                @pl.when((h > 0) & (h <= hops(n, way)))
                def _():
                    rs_copy(n, way, h - 1).wait_recv()

                    @pl.when(h < hops(n, way))
                    def _():
                        step = hops(n, way) - h
                        own = chip_at(q + step if way == 0 else q - step)
                        total = W[slot, own].astype(F32) + R[came(n, way, h - 1)].astype(F32)
                        W[slot, own] = total.astype(BF16)
                        rs_copy(n, way, h).start()

            @pl.when(h == 4)
            def _():
                total = W[slot, chip].astype(F32) + R[came(n, 0, hops(n, 0) - 1)].astype(F32)
                total = total + R[came(n, 1, hops(n, 1) - 1)].astype(F32)
                W[slot, chip] = total.astype(BF16)

                @pl.when(kind(n) == 2)
                def _():
                    out_down(n).start()

                @pl.when(kind(n) != 2)
                def _():
                    out_here(n).start()
                    out_there(n).start()

                @pl.when(n < ALL - R_SLOTS)
                def _():
                    for way in (0, 1):
                        pl.semaphore_signal(credit.at[way], inc=1, device_id=ring[1 - way], device_id_type=MESH)

    def rs_events(lo, hi):
        def body(e, _):
            rs_event(e // 5, 4 - lax.rem(e, 5))
            return 0

        lax.fori_loop(lo, hi, body, 0)

    block = min(256, tok)
    blocks = 2 * tok // block

    def part(t, size=block):
        return pl.ds(pl.multiple_of(t * size, size), size)

    def normed(h):
        wide = h.astype(F32)
        return (wide * lax.rsqrt(jnp.mean(wide * wide, -1, keepdims=True) + 1e-6)).astype(BF16)

    def norm_block(c, flip):
        def body(t, _):
            s = pl.ds(pl.multiple_of(c * tok + t * block, block), block)
            a = normed(A[s, :])
            A[s, :] = a
            if flip:
                AT[:, s] = a.T
            return 0

        lax.fori_loop(0, tok // block, body, 0)

    def flip_dy(c):
        def body(t, _):
            s = pl.ds(pl.multiple_of(c * tok + t * block, block), block)
            DYT[:, s] = DY[s, :].T
            return 0

        lax.fori_loop(0, tok // block, body, 0)

    def clear():
        def body(t, _):
            ACC[part(t), :] = jnp.zeros((block, d), F32)
            return 0

        lax.fori_loop(0, blocks, body, 0)

    def own_block(t):
        return pl.ds(pl.multiple_of(core * tok + t * block, block), block)

    def nth(t):
        return part(lax.rem(t + 2 * (1 - core), 4), tile)

    def swap(k, t):
        src = ACC.at[pl.ds(pl.multiple_of((1 - core) * tok + t * tile, tile), tile)]
        return remote(src, PT.at[part(t, tile)], sw_send.at[k, t], sw_recv.at[k, t], mate)

    def forward(j, after):
        i, hh = j // 2, lax.rem(j, 2)
        r = 3 * i + 1 + hh

        def body(t, _):
            s = nth(t)
            at = A[s, :]
            gate = nn(at, W[r, :, 0].reshape(d, -1))
            up = nn(at, W[r, :, 1].reshape(d, -1))
            act = (gate * (0.5 * jnp.tanh(0.5 * gate) + 0.5) * up).astype(BF16)
            ACC[s, :] += nn(act, W[3 * i, pl.ds(4 * hh, 4)].reshape(-1, d))

            @pl.when((j == 7) & (t < 2))
            def _():
                swap(0, t).start()

            after(t)
            return 0

        lax.fori_loop(0, 4, body, 0)

    ag_events(0, 5)
    prep_all(3, ROUNDS)
    loaded_up(1)
    prep_all(ROUNDS, ALL)
    load_x.wait()
    norm_block(core, False)
    ag_events(5, 9)
    send_x.wait_recv()
    norm_block(1 - core, False)
    clear()
    ag_events(9, 15)
    load_dy.wait()
    flip_dy(core)
    ag_events(15, 20)
    send_dy.wait_recv()
    flip_dy(1 - core)
    ag_events(20, 27)

    def first(j, _):
        i, hh = j // 2, lax.rem(j, 2)

        @pl.when(hh == 0)
        def _():
            ag_ready(3 * i)

        ag_ready(3 * i + 1 + hh)
        lo = 27 + (15 * j) // 2
        count = 27 + (15 * (j + 1)) // 2 - lo
        forward(j, lambda t: ag_events(lo + (count * t) // 4, lo + (count * (t + 1)) // 4))
        return 0

    lax.fori_loop(0, 8, first, 0)

    whole = DG.at[pl.ds(0, 4 * ALL // 3 * rows)]
    remote(whole, whole, prep_send, prep_rem.at[0], mate).wait_send()
    fetch = pltpu.make_async_copy(x_ref, DG.at[pl.ds(0, tok)], loc.at[2])
    fetch.start()
    ag_events(87, 90)
    fetch.wait()
    swap(0, 0).wait()
    swap(0, 1).wait()

    def residual(t, _):
        mlp = (ACC[own_block(t), :] + PT[part(t), :]).astype(BF16)
        h = (DG[part(t), :].astype(F32) + mlp.astype(F32)).astype(BF16)
        ACT[part(t), :] = h
        A[own_block(t), :] = h
        return 0

    lax.fori_loop(0, tok // block, residual, 0)
    h1 = ACT.at[pl.ds(0, tok)]
    send_h = remote(h1, A.at[mine], ex_send.at[3], ex_recv.at[3], mate)
    keep_h = pltpu.make_async_copy(h1, h1_ref, loc.at[3])
    send_h.start()
    keep_h.start()
    clear()
    norm_block(core, True)
    ag_events(90, 95)
    send_h.wait()
    norm_block(1 - core, True)
    ag_events(95, 100)
    keep_h.wait()

    def norm_back(h_ref, t):
        by_a = (ACC[own_block(t), :] + PT[part(t), :]).astype(BF16).astype(F32)
        wide = h_ref[part(t), :].astype(F32)
        scale = lax.rsqrt(jnp.mean(wide * wide, -1, keepdims=True) + 1e-6)
        along = jnp.mean(by_a * wide, -1, keepdims=True)
        by_h = (by_a * scale - wide * (scale * scale * scale * along)).astype(BF16)
        return (DY[own_block(t), :].astype(F32) + by_h.astype(F32)).astype(BF16)

    def chunk(c, _):
        l = 1 - c // 8
        j = lax.rem(c, 8)
        i, hh = j // 2, lax.rem(j, 2)
        pair = c // 2
        base = ROUNDS * l + 3 * i
        up_slot, down_slot = term(3 * pair + hh), term(3 * pair + 2)

        lo = jnp.where(c == 8, BETWEEN[1], events_by(c))
        count = events_by(c + 1) - lo

        def serve(slot):
            ag_lo, ag_hi = 100 + 10 * c + (10 * slot) // 8, 100 + 10 * c + (10 * slot + 10) // 8
            ag_events(jnp.minimum(ag_lo, 140), jnp.minimum(ag_hi, 140))
            rs_events(lo + (count * slot) // 8, lo + (count * slot + count) // 8)

        @pl.when(c == 8)
        def _():
            start, end = BETWEEN
            again = pltpu.make_async_copy(x_ref, A.at[mine], loc.at[5])
            again.start()
            send_xp.wait_recv()
            other = pltpu.make_async_copy(xp_ref, A.at[theirs], loc.at[6])
            other.start()
            fetch = pltpu.make_async_copy(h1_ref, DG.at[pl.ds(0, tok)], loc.at[4])
            fetch.start()
            rs_events(start, start + 1)
            fetch.wait()
            swap(1, 0).wait()
            swap(1, 1).wait()

            def body(t, _):
                dh = norm_back(DG, t)
                DY[own_block(t), :] = dh
                ACT[part(t), :] = dh
                return 0

            lax.fori_loop(0, tok // block, body, 0)
            send = remote(ACT.at[pl.ds(0, tok)], DY.at[mine], ex_send.at[4], ex_recv.at[4], mate)
            send.start()
            clear()
            flip_dy(core)
            rs_events(start + 1, start + 2)
            again.wait()
            norm_block(core, True)
            rs_events(start + 2, start + 3)
            other.wait()
            norm_block(1 - core, True)
            rs_events(start + 3, end)
            send.wait()
            flip_dy(1 - core)

            def gone(r, _):
                ag_retire(r)
                return 0

            lax.fori_loop(ALL - S_SLOTS, ALL, gone, 0)
            across_sent(1)

        @pl.when(l == 1)
        def _():
            @pl.when(hh == 0)
            def _():
                ag_ready(base)

            ag_ready(base + 1 + hh)

        def tokens(t, _):
            s = nth(t)
            at = A[s, :]
            wg, wu = W[base + 1 + hh, :, 0].reshape(d, -1), W[base + 1 + hh, :, 1].reshape(d, -1)
            gate, up = nn(at, wg), nn(at, wu)
            by_act = nt(DY[s, :], W[base, pl.ds(4 * hh, 4)].reshape(-1, d)).astype(BF16).astype(F32)
            sig = 0.5 * jnp.tanh(0.5 * gate) + 0.5
            silu = gate * sig
            ACT[s, :] = (silu * up).astype(BF16)
            dup = (by_act * silu).astype(BF16)
            dgate = (by_act * up * (sig + silu * (1.0 - sig))).astype(BF16)
            DG[s, :] = dgate
            DU[s, :] = dup
            ACC[s, :] += nt(dgate, wg) + nt(dup, wu)

            @pl.when((j == 7) & (t < 2))
            def _():
                swap(2 - l, t).start()

            serve(t)
            return 0

        lax.fori_loop(0, 4, tokens, 0)

        for back, when in ((0, 0), (1, 1), (2, 0)):
            n = 3 * pair + back - T_SLOTS

            @pl.when((hh == when) & (n >= 0))
            def _():
                rs_retire(n)

        def grads_up(p, _):
            s = pl.ds(pl.multiple_of(p * (d // 2), d // 2), d // 2)
            W[up_slot, pl.ds(4 * p, 4), 0] = nn(AT[s, :], DG[...]).astype(BF16).reshape(4, half, -1)
            W[up_slot, pl.ds(4 * p, 4), 1] = nn(AT[s, :], DU[...]).astype(BF16).reshape(4, half, -1)
            serve(4 + p)
            return 0

        lax.fori_loop(0, 2, grads_up, 0)

        for p in range(2):
            s = slice(p * (d // 2), (p + 1) * (d // 2))
            g = nn(DYT[s, :], ACT[...]).T.astype(BF16)
            W[down_slot, pl.ds(4 * hh, 4), :, :, s] = g.reshape(4, 2, half, d // 2)
            serve(6 + p)

        return 0

    lax.fori_loop(0, 16, chunk, 0)

    fetch = pltpu.make_async_copy(x_ref, DG.at[pl.ds(0, tok)], loc.at[7])
    fetch.start()
    rs_events(114, 115)
    fetch.wait()
    swap(2, 0).wait()
    swap(2, 1).wait()

    def last(t, _):
        ACT[part(t), :] = norm_back(DG, t)
        return 0

    lax.fori_loop(0, tok // block, last, 0)
    put = pltpu.make_async_copy(ACT.at[pl.ds(0, tok)], dx_ref, loc.at[8])
    put.start()
    rs_events(115, 140)

    put.wait()
    for copy in (send_x, send_xp, send_dy):
        copy.wait_send()

    def sent(r, _):
        @pl.when(r >= ALL - T_SLOTS)
        def _():
            rs_retire(r)

        @pl.when(kind(r) != 2)
        def _():
            out_there(r).wait_recv()

        return 0

    across_sent(0)
    lax.fori_loop(0, ALL, sent, 0)


def put_kernel(dx_ref, og_ref, od_ref, dx_out, dwg_out, dwu_out, dwd_out, dx, og, od, dwg, dwu, came, went):
    layers = dwg.shape[0]
    strip = dwg.shape[2] // 64
    loads = [pltpu.make_async_copy(og_ref.at[l], og.at[l], came.at[l]) for l in range(layers)]
    others = [(dx_ref, dx, dx_out), (od_ref, od, dwd_out)]
    for copy in loads:
        copy.start()
    for k, (src, buffer, _) in enumerate(others):
        pltpu.make_async_copy(src, buffer, came.at[2 + k]).start()
    for l in range(layers):
        loads[l].wait()
        for part in range(16):
            c, i, hh = part // 8, part // 2 % 4, part % 2
            for s in range(4):
                column = strip * (8 * (4 * hh + s) + 4 * c + i)
                for g, out in enumerate((dwg, dwu)):
                    out[l, :, column : column + strip] = og[l, c, i, hh, g, :, strip * s : strip * (s + 1)]
        pltpu.make_async_copy(dwg.at[l], dwg_out.at[l], went.at[2 * l]).start()
        pltpu.make_async_copy(dwu.at[l], dwu_out.at[l], went.at[2 * l + 1]).start()
    for k, (src, buffer, dst) in enumerate(others):
        pltpu.make_async_copy(src, buffer, came.at[2 + k]).wait()
        pltpu.make_async_copy(buffer, dst, went.at[4 + k]).start()
    for l in range(layers):
        pltpu.make_async_copy(dwg.at[l], dwg_out.at[l], went.at[2 * l]).wait()
        pltpu.make_async_copy(dwu.at[l], dwu_out.at[l], went.at[2 * l + 1]).wait()
    for k, (_, buffer, dst) in enumerate(others):
        pltpu.make_async_copy(buffer, dst, went.at[4 + k]).wait()


def of_a_device(x, dy, w_gate, w_up, w_down):
    _, tok, d = x.shape
    layers, rows, ff = w_gate.shape
    half = 2 * rows
    strip = ff // 64
    wd = w_down.reshape(layers, 4, 2, half, d)
    hbm = pl.BlockSpec(memory_space=pltpu.HBM)
    tile = tok // 2
    piece = (2, half, d)
    both = 2 * tok
    dma = pltpu.SemaphoreType.DMA
    up = (layers, 2, 4, 2, 2, rows, 4 * strip)
    dx, og, od, _, _ = pl.pallas_call(
        functools.partial(kernel, tile),
        out_shape=tuple(
            jax.ShapeDtypeStruct(shape, BF16)
            for shape in ((tok, d), up, wd.shape, (tok, d), (tok, d))
        ),
        in_specs=[hbm] * 5,
        out_specs=[hbm] * 5,
        scratch_shapes=[
            pltpu.VMEM((ALL + T_SLOTS, 8, *piece), BF16),
            pltpu.VMEM((7 * R_SLOTS, *piece), BF16),
            pltpu.VMEM((both, d), BF16),
            pltpu.VMEM((d, both), BF16),
            pltpu.VMEM((both, d), BF16),
            pltpu.VMEM((d, both), BF16),
            pltpu.VMEM((both, d), F32),
            pltpu.VMEM((tok, d), F32),
            pltpu.VMEM((both, 4 * strip), BF16),
            pltpu.VMEM((both, 4 * strip), BF16),
            pltpu.VMEM((both, 4 * strip), BF16),
            dma((ALL // 3,)),
            dma((layers,)),
            dma(()),
            dma((2 * ALL // 3,)),
            dma((S_SLOTS, 2)),
            dma((S_SLOTS, 2, 4)),
            dma((2,)),
            dma((ALL,)),
            dma((T_SLOTS, 2)),
            dma((R_SLOTS, 2, 4)),
            dma((T_SLOTS,)),
            dma((T_SLOTS,)),
            dma((2 * ALL // 3,)),
            dma((5,)),
            dma((5,)),
            dma((3, 2)),
            dma((3, 2)),
            dma((9,)),
            pltpu.SemaphoreType.REGULAR((2,)),
        ],
        compiler_params=pltpu.CompilerParams(
            collective_id=0, has_side_effects=True, vmem_limit_bytes=67043328
        ),
    )(x[0], dy[0], w_gate, w_up, wd)
    results = (dx.shape, w_gate.shape, w_up.shape, od.shape)
    dx, dwg, dwu, dwd = pl.pallas_call(
        put_kernel,
        out_shape=tuple(jax.ShapeDtypeStruct(shape, BF16) for shape in results),
        in_specs=[hbm] * 3,
        out_specs=[hbm] * 4,
        scratch_shapes=[
            *(pltpu.VMEM(shape, BF16) for shape in (dx.shape, up, od.shape, w_gate.shape, w_up.shape)),
            dma((4,)),
            dma((6,)),
        ],
    )(dx, og, od)
    return dx[None], dwg, dwu, dwd.reshape(w_down.shape)


def solution(mesh):
    by_seq, by_row = P(("rep", "dp"), None, None), P(None, "dp", None)
    out = P("rep", "dp", None)
    return jax.shard_map(
        of_a_device,
        mesh=mesh,
        in_specs=(by_seq, by_seq, by_row, by_row, by_row),
        out_specs=(by_seq, out, out, out),
        check_vma=False,
    )
```

time: 458 us -> 418 us (0.913)
  Pallas kernels: 436 us -> 418 us
  local copies, waits for them, and re-layouts: 17.5 us -> 0 us
    pallas_call x1 -> x2, Pallas kernels: 436 us -> 418 us  [the longest x1 414 us: of_a_device(): pl.pallas_call(functools.partial(kernel, tile), out_shape=tuple((jax.Shap...]
    reshape x2 -> x0, local copies, waits for them, and re-layouts: 4.77 us -> none  [the longest x1 2.55 us: of_a_device(): og = og.reshape(layers, 2, 4, 2, 2, rows, 4, strip)]
where the time goes in v2:
time: 418 us
  Pallas kernels  418 us (100%)
    pallas_call x1, Pallas kernels, of_a_device(): pl.pallas_call(functools.partial(kernel, tile), out_shape=tuple((jax.Shap...  414 us

profile of v2, /device:TPU:0, one launch (start us, length us, event | category | flops | bytes accessed | tf_op | source)
XLA Modules:
  0.0 418.2 jit_solution(5486022387934028924)
XLA Ops:
  0.6 414.0 %shard_map.84 = (bf16[1024,512]{1,0:T(8,128)(2,1)}, bf16[2,2,4,2,2,32,512]{6,5,4,3,2,1,0:T(8,128)(2,1)}, bf16[2,4,2,64,512]{4,3,2,1,0:T(8,128)(2,1)}, bf16[1024,512]{1,0:T(8,128)(2,1)}, bf16[1024,512]{1,0:T(8,128)(2,1)}) custom-call(bf16[1024,512]{1,0:T(8,128)(2,1)} %bitcast.5, bf16[1024,512]{1,0:T(8,128)(2,1)} %bitcast.6, bf16[2,32,8192]{2,1,0:T(8,128)(2,1)} %wg_ref.1, ...), custom_call_target="tpu_custom_call" | custom-call | tf_op jit(solution)/shard_map/pallas_call | solution.py:661
  414.6 3.6 shard_map.85

commit v3 on v2

--- a/solution.py
+++ b/solution.py
@@ -12,11 +12,21 @@
 ROUNDS = 12
 ALL = 2 * ROUNDS
 T_SLOTS, R_SLOTS, S_SLOTS = 8, 6, 8
-BETWEEN = 48, 54
+GATHERED = 14
+FIRST = (21, 27, 31, 37, 41, 47, 50, 52, 55)
+BETWEEN = 44, 50
+LAST_AG, LAST_RS = 5 * (GATHERED - 1) + 17, 5 * (ALL - 1) + 17
 
 
 def events_by(c):
-    return jnp.where(c <= 8, jnp.maximum((13 * c - 8) // 2, 0), (15 * c - 11) // 2)
+    return jnp.where(c <= 8, jnp.maximum((13 * c - 16) // 2, 0), (15 * c - 19) // 2)
+
+
+def pick(values, k):
+    out = values[-1]
+    for number, value in enumerate(values[:-1]):
+        out = jnp.where(k == number, value, out)
+    return out
 
 
 def nn(a, b):
@@ -156,55 +166,61 @@
 
     def gathers(r):
         first = (kind(r) == 2) | (kind(r) == rep)
-        return jnp.where(r < ROUNDS, first, lax.rem(r, 2) == rep)
-
-    def ag_copy(r, way, h):
+        return jnp.where(r < ROUNDS, first, (r - ROUNDS) // 6 == rep)
+
+    def gathered(g):
+        return jnp.where(
+            g < 8, pick((rep, 3 + rep, 2, 6 + rep, 5, 9 + rep, 8, 11), g), ROUNDS + 6 * rep + g - 8
+        )
+
+    def ag_copy(g, r, way, h):
         piece = W.at[r, chip_at(q - h if way == 0 else q + h)]
-        return remote(piece, piece, ag_send.at[lax.rem(r, S_SLOTS), way], ag_recv.at[lax.rem(r, S_SLOTS), way, h], ring[way])
-
-    def ag_retire(r):
+        slot = lax.rem(g, S_SLOTS)
+        return remote(piece, piece, ag_send.at[slot, way], ag_recv.at[slot, way, h], ring[way])
+
+    def ag_retire(g):
         for way in (0, 1):
             for count in (3, 4):
-                @pl.when(gathers(r) & (hops(r, way) == count))
-                def _():
-                    sent = W.at[r, pl.ds(0, count)]
-                    remote(sent, sent, ag_send.at[lax.rem(r, S_SLOTS), way], ag_recv.at[0, way, 0], ring[way]).wait_send()
-
-    def ag_event(n, h):
-        r = n - h
-        ok = (r >= 0) & (r < ALL)
-
-        @pl.when(ok & (h == 0))
-        def _():
-            wait_prep(r)
-
-            @pl.when(r >= S_SLOTS)
+                @pl.when(hops(g, way) == count)
+                def _():
+                    sent = W.at[0, pl.ds(0, count)]
+                    remote(sent, sent, ag_send.at[lax.rem(g, S_SLOTS), way], ag_recv.at[0, way, 0], ring[way]).wait_send()
+
+    def ag_event(g, h):
+        @pl.when((g >= 0) & (g < GATHERED))
+        def _():
+            r = gathered(g)
+
+            @pl.when(h == 0)
             def _():
-                ag_retire(r - S_SLOTS)
-
-        @pl.when(ok & gathers(jnp.maximum(r, 0)))
-        def _():
+                wait_prep(r)
+
+                @pl.when(g >= S_SLOTS)
+                def _():
+                    ag_retire(g - S_SLOTS)
+
             for way in (0, 1):
                 @pl.when(h == 0)
                 def _():
-                    ag_copy(r, way, 0).start()
-
-                @pl.when((h > 0) & (h <= hops(r, way)))
-                def _():
-                    piece = W.at[r, chip_at(q - h if way == 0 else q + h)]
-                    ag_copy(r, way, h - 1).wait_recv()
-
-                    @pl.when(h < hops(r, way))
+                    ag_copy(g, r, way, 0).start()
+
+                @pl.when((h > 0) & (h <= hops(g, way)))
+                def _():
+                    ag_copy(g, r, way, h - 1).wait_recv()
+
+                    @pl.when(h < hops(g, way))
                     def _():
-                        ag_copy(r, way, h).start()
+                        ag_copy(g, r, way, h).start()
 
                     @pl.when(shared(r))
                     def _():
+                        piece = W.at[r, chip_at(q - h if way == 0 else q + h)]
                         remote(piece, piece, ax_send.at[r // ROUNDS], ax_recv.at[r], across).start()
 
     def ag_ready(r):
         @pl.when(jnp.logical_not(gathers(r)))
         def _():
+            wait_prep(r)
             seven = W.at[r, pl.ds(0, 7)]
             remote(seven, seven, ax_send.at[0], ax_recv.at[r], across).wait_recv()
 
@@ -214,10 +230,17 @@
 
     def ag_events(lo, hi):
         def body(e, _):
-            ag_event(e // 5, 4 - lax.rem(e, 5))
+            h = lax.rem(4 * e, 5)
+            ag_event((e - 4 * h) // 5, h)
             return 0
 
         lax.fori_loop(lo, hi, body, 0)
+
+    def turn(l, k):
+        return jnp.where(l == 1, lax.rem(k + 2 * rep, 4), k)
+
+    def strip_of(n):
+        return turn(1 - n // ROUNDS, lax.rem(n, ROUNDS) // 3)
 
     def term(n):
         return jnp.where(n < ROUNDS, ALL + lax.rem(n, T_SLOTS), n)
@@ -241,11 +264,11 @@
 
     def out_down(n):
         return pltpu.make_async_copy(
-            W.at[term(n), chip], od_ref.at[1 - n // ROUNDS, lax.rem(n, ROUNDS) // 3], out_loc.at[own_sem(n)]
+            W.at[term(n), chip], od_ref.at[1 - n // ROUNDS, strip_of(n)], out_loc.at[own_sem(n)]
         )
 
     def out_up(n):
-        return og_ref.at[1 - n // ROUNDS, core, lax.rem(n, ROUNDS) // 3, jnp.minimum(kind(n), 1)]
+        return og_ref.at[1 - n // ROUNDS, core, strip_of(n), jnp.minimum(kind(n), 1)]
 
     def out_here(n):
         return pltpu.make_async_copy(W.at[term(n), chip, :, own_rows], out_up(n), out_loc.at[own_sem(n)])
@@ -272,8 +295,7 @@
             out_here(n).wait()
             out_there(n).wait_send()
 
-    def rs_event(n0, h):
-        n = n0 - h
+    def rs_event(n, h):
         ok = (n >= 0) & (n < ALL)
 
         @pl.when(ok)
@@ -322,7 +344,8 @@
 
     def rs_events(lo, hi):
         def body(e, _):
-            rs_event(e // 5, 4 - lax.rem(e, 5))
+            h = lax.rem(4 * e, 5)
+            rs_event((e - 4 * h) // 5, h)
             return 0
 
         lax.fori_loop(lo, hi, body, 0)
@@ -394,23 +417,24 @@
 
         lax.fori_loop(0, 4, body, 0)
 
-    ag_events(0, 5)
+    ag_events(0, 1)
     prep_all(3, ROUNDS)
+    ag_events(1, 4)
     loaded_up(1)
     prep_all(ROUNDS, ALL)
     load_x.wait()
     norm_block(core, False)
-    ag_events(5, 9)
+    ag_events(4, 6)
     send_x.wait_recv()
     norm_block(1 - core, False)
     clear()
-    ag_events(9, 15)
+    ag_events(6, 9)
     load_dy.wait()
     flip_dy(core)
-    ag_events(15, 20)
+    ag_events(9, 11)
     send_dy.wait_recv()
     flip_dy(1 - core)
-    ag_events(20, 27)
+    ag_events(11, FIRST[0])
 
     def first(j, _):
         i, hh = j // 2, lax.rem(j, 2)
@@ -420,8 +444,7 @@
             ag_ready(3 * i)
 
         ag_ready(3 * i + 1 + hh)
-        lo = 27 + (15 * j) // 2
-        count = 27 + (15 * (j + 1)) // 2 - lo
+        lo, count = pick(FIRST[:8], j), pick(FIRST[1:], j) - pick(FIRST[:8], j)
         forward(j, lambda t: ag_events(lo + (count * t) // 4, lo + (count * (t + 1)) // 4))
         return 0
 
@@ -431,7 +454,7 @@
     remote(whole, whole, prep_send, prep_rem.at[0], mate).wait_send()
     fetch = pltpu.make_async_copy(x_ref, DG.at[pl.ds(0, tok)], loc.at[2])
     fetch.start()
-    ag_events(87, 90)
+    ag_events(55, 57)
     fetch.wait()
     swap(0, 0).wait()
     swap(0, 1).wait()
@@ -451,10 +474,10 @@
     keep_h.start()
     clear()
     norm_block(core, True)
-    ag_events(90, 95)
+    ag_events(57, 60)
     send_h.wait()
     norm_block(1 - core, True)
-    ag_events(95, 100)
+    ag_events(60, 62)
     keep_h.wait()
 
     def norm_back(h_ref, t):
@@ -468,7 +491,7 @@
     def chunk(c, _):
         l = 1 - c // 8
         j = lax.rem(c, 8)
-        i, hh = j // 2, lax.rem(j, 2)
+        i, hh = turn(l, j // 2), lax.rem(j, 2)
         pair = c // 2
         base = ROUNDS * l + 3 * i
         up_slot, down_slot = term(3 * pair + hh), term(3 * pair + 2)
@@ -477,8 +500,8 @@
         count = events_by(c + 1) - lo
 
         def serve(slot):
-            ag_lo, ag_hi = 100 + 10 * c + (10 * slot) // 8, 100 + 10 * c + (10 * slot + 10) // 8
-            ag_events(jnp.minimum(ag_lo, 140), jnp.minimum(ag_hi, 140))
+            ag_lo, ag_hi = 62 + 8 * c + slot, 63 + 8 * c + slot
+            ag_events(jnp.minimum(ag_lo, LAST_AG), jnp.minimum(ag_hi, LAST_AG))
             rs_events(lo + (count * slot) // 8, lo + (count * slot + count) // 8)
 
         @pl.when(c == 8)
@@ -517,11 +540,11 @@
             send.wait()
             flip_dy(1 - core)
 
-            def gone(r, _):
-                ag_retire(r)
+            def gone(g, _):
+                ag_retire(g)
                 return 0
 
-            lax.fori_loop(ALL - S_SLOTS, ALL, gone, 0)
+            lax.fori_loop(GATHERED - S_SLOTS, GATHERED, gone, 0)
             across_sent(1)
 
         @pl.when(l == 1)
@@ -584,7 +607,7 @@
 
     fetch = pltpu.make_async_copy(x_ref, DG.at[pl.ds(0, tok)], loc.at[7])
     fetch.start()
-    rs_events(114, 115)
+    rs_events(110, 111)
     fetch.wait()
     swap(2, 0).wait()
     swap(2, 1).wait()
@@ -596,7 +619,7 @@
     lax.fori_loop(0, tok // block, last, 0)
     put = pltpu.make_async_copy(ACT.at[pl.ds(0, tok)], dx_ref, loc.at[8])
     put.start()
-    rs_events(115, 140)
+    rs_events(111, LAST_RS)
 
     put.wait()
     for copy in (send_x, send_xp, send_dy):

time: 418 us -> 403 us (0.964)
  Pallas kernels: 418 us -> 402 us
    pallas_call x1, Pallas kernels: 414 us -> 399 us  [of_a_device(): pl.pallas_call(functools.partial(kernel, tile), out_shape=tuple((jax.Shap...]
where the time goes in v3:
time: 403 us
  Pallas kernels  402 us (100%)
    pallas_call x1, Pallas kernels, of_a_device(): pl.pallas_call(functools.partial(kernel, tile), out_shape=tuple((jax.Shap...  399 us

profile of v3, /device:TPU:0, one launch (start us, length us, event | category | flops | bytes accessed | tf_op | source)
XLA Modules:
  0.0 403.0 jit_solution(12343757836676659466)
XLA Ops:
  0.6 398.8 %shard_map.84 = (bf16[1024,512]{1,0:T(8,128)(2,1)}, bf16[2,2,4,2,2,32,512]{6,5,4,3,2,1,0:T(8,128)(2,1)}, bf16[2,4,2,64,512]{4,3,2,1,0:T(8,128)(2,1)}, bf16[1024,512]{1,0:T(8,128)(2,1)}, bf16[1024,512]{1,0:T(8,128)(2,1)}) custom-call(bf16[1024,512]{1,0:T(8,128)(2,1)} %bitcast.5, bf16[1024,512]{1,0:T(8,128)(2,1)} %bitcast.6, bf16[2,32,8192]{2,1,0:T(8,128)(2,1)} %wg_ref.1, ...), custom_call_target="tpu_custom_call" | custom-call | tf_op jit(solution)/shard_map/pallas_call | solution.py:684
  399.4 3.6 shard_map.85

commit v4 on v3

--- a/solution.py
+++ b/solution.py
@@ -14,12 +14,13 @@
 T_SLOTS, R_SLOTS, S_SLOTS = 8, 6, 8
 GATHERED = 14
 FIRST = (21, 27, 31, 37, 41, 47, 50, 52, 55)
-BETWEEN = 44, 50
-LAST_AG, LAST_RS = 5 * (GATHERED - 1) + 17, 5 * (ALL - 1) + 17
+BETWEEN = 45, 51
+SECOND = (62, 67, 77, 82, 82)
+LAST_AG, LAST_RS = 5 * (GATHERED - 1) + 17, 5 * ALL + 17
 
 
 def events_by(c):
-    return jnp.where(c <= 8, jnp.maximum((13 * c - 16) // 2, 0), (15 * c - 19) // 2)
+    return jnp.where(c <= 8, jnp.maximum((13 * c - 14) // 2, jnp.minimum(c, 1)), (15 * c - 19) // 2)
 
 
 def pick(values, k):
@@ -27,6 +28,14 @@
     for number, value in enumerate(values[:-1]):
         out = jnp.where(k == number, value, out)
     return out
+
+
+def loop(end, body, start=0):
+    def step(k, carry):
+        body(k)
+        return carry
+
+    lax.fori_loop(start, end, step, 0)
 
 
 def nn(a, b):
@@ -82,13 +91,12 @@
         return 8 * l + spot // 4, lax.rem(spot // 2, 2), pl.ds(pl.multiple_of(rows * lax.rem(spot, 2), rows), rows), columns
 
     def load_up(l):
-        def body(b, _):
+        def body(b):
             for g, ref in enumerate((wg_ref, wu_ref)):
                 src = ref.at[l, :, pl.ds(pl.multiple_of(d * b, d), d)]
                 pltpu.make_async_copy(src, R.at[staged(l, g, b)], prep_up.at[l]).start()
-            return 0
-
-        lax.fori_loop(0, 16, body, 0)
+
+        loop(16, body)
 
     def loaded_up(l):
         eight = R.at[pl.ds(8 * l, 8)]
@@ -116,23 +124,20 @@
         part = W.at[r, chip, :, own_rows]
         return remote(part, part, prep_send, prep_rem.at[up_number(r)], mate)
 
-    def prep_first(r, _):
+    def prep_first(r):
         prep_down(3 * r).start()
-        return 0
 
     load_up(0)
-    lax.fori_loop(0, ALL // 3, prep_first, 0)
+    loop(ALL // 3, prep_first)
     load_up(1)
 
     def prep_all(lo, hi):
-        def body(r, _):
+        def body(r):
             @pl.when(kind(r) != 0)
             def _():
                 prep_start(r)
 
-            return 0
-
-        lax.fori_loop(lo, hi, body, 0)
+        loop(hi, body, lo)
 
     load_x = pltpu.make_async_copy(x_ref, A.at[mine], loc.at[0])
     load_dy = pltpu.make_async_copy(dy_ref, DY.at[mine], loc.at[1])
@@ -168,6 +173,9 @@
         first = (kind(r) == 2) | (kind(r) == rep)
         return jnp.where(r < ROUNDS, first, (r - ROUNDS) // 6 == rep)
 
+    def across_number(r):
+        return jnp.where(r < ROUNDS, r // 3, 4 + lax.rem(r, 6))
+
     def gathered(g):
         return jnp.where(
             g < 8, pick((rep, 3 + rep, 2, 6 + rep, 5, 9 + rep, 8, 11), g), ROUNDS + 6 * rep + g - 8
@@ -215,26 +223,25 @@
                     @pl.when(shared(r))
                     def _():
                         piece = W.at[r, chip_at(q - h if way == 0 else q + h)]
-                        remote(piece, piece, ax_send.at[r // ROUNDS], ax_recv.at[r], across).start()
+                        remote(piece, piece, ax_send.at[r // ROUNDS], ax_recv.at[across_number(r)], across).start()
 
     def ag_ready(r):
         @pl.when(jnp.logical_not(gathers(r)))
         def _():
             wait_prep(r)
             seven = W.at[r, pl.ds(0, 7)]
-            remote(seven, seven, ax_send.at[0], ax_recv.at[r], across).wait_recv()
+            remote(seven, seven, ax_send.at[0], ax_recv.at[across_number(r)], across).wait_recv()
 
     def across_sent(l):
         some = W.at[pl.ds(0, 7), pl.ds(0, 4)] if l == 0 else W.at[pl.ds(0, 7), pl.ds(0, 6)]
         remote(some, some, ax_send.at[l], ax_recv.at[0], across).wait_send()
 
     def ag_events(lo, hi):
-        def body(e, _):
+        def body(e):
             h = lax.rem(4 * e, 5)
             ag_event((e - 4 * h) // 5, h)
-            return 0
-
-        lax.fori_loop(lo, hi, body, 0)
+
+        loop(hi, body, lo)
 
     def turn(l, k):
         return jnp.where(l == 1, lax.rem(k + 2 * rep, 4), k)
@@ -248,24 +255,26 @@
     def own_sem(n):
         return lax.rem(n, T_SLOTS)
 
-    def came(n, way, h):
-        return 7 * lax.rem(n, R_SLOTS) + (h if way == 0 else hops(n, 0) + h)
-
-    def rs_copy(n, way, h):
-        slot = own_sem(n)
+    def spot(n, owner, cut):
+        return (ALL - 1, owner, n - (ALL - 1)) if cut else (term(n), owner)
+
+    def came(n, way, h, cut):
+        place = 7 * lax.rem(n, R_SLOTS) + (h if way == 0 else hops(n, 0) + h)
+        return (place, 0) if cut else (place,)
+
+    def rs_copy(n, way, h, cut):
         step = hops(n, way) - h
         return remote(
-            W.at[term(n), chip_at(q + step if way == 0 else q - step)],
-            R.at[came(n, way, h)],
-            rs_send.at[slot, way],
+            W.at[spot(n, chip_at(q + step if way == 0 else q - step), cut)],
+            R.at[came(n, way, h, cut)],
+            rs_send.at[own_sem(n), way],
             rs_recv.at[lax.rem(n, R_SLOTS), way, h],
             ring[way],
         )
 
-    def out_down(n):
-        return pltpu.make_async_copy(
-            W.at[term(n), chip], od_ref.at[1 - n // ROUNDS, strip_of(n)], out_loc.at[own_sem(n)]
-        )
+    def out_down(n, cut):
+        dst = (0, 3, n - (ALL - 1)) if cut else (1 - n // ROUNDS, strip_of(n))
+        return pltpu.make_async_copy(W.at[spot(n, chip, cut)], od_ref.at[dst], out_loc.at[own_sem(n)])
 
     def out_up(n):
         return og_ref.at[1 - n // ROUNDS, core, strip_of(n), jnp.minimum(kind(n), 1)]
@@ -275,80 +284,90 @@
 
     def out_there(n):
         part = W.at[term(n), chip, :, mate_rows]
-        number = 2 * (n // 3) + jnp.minimum(kind(n), 1)
-        return remote(part, out_up(n), out_send.at[own_sem(n)], out_recv.at[number], mate)
-
-    def rs_retire(n):
+        return remote(part, out_up(n), out_send.at[own_sem(n)], out_recv, mate)
+
+    def rs_retire(n, cut=False):
         for way in (0, 1):
             for count in (3, 4):
                 @pl.when(hops(n, way) == count)
                 def _():
-                    sent = W.at[term(n), pl.ds(0, count)]
+                    sent = W.at[spot(n, pl.ds(0, count), cut)]
                     remote(sent, sent, rs_send.at[own_sem(n), way], rs_recv.at[0, way, 0], ring[way]).wait_send()
 
+        if cut:
+            out_down(n, cut).wait()
+            return
+
         @pl.when(kind(n) == 2)
         def _():
-            out_down(n).wait()
+            out_down(n, cut).wait()
 
         @pl.when(kind(n) != 2)
         def _():
             out_here(n).wait()
             out_there(n).wait_send()
 
-    def rs_event(n, h):
-        ok = (n >= 0) & (n < ALL)
-
-        @pl.when(ok)
-        def _():
-            slot = term(n)
-            for way in (0, 1):
-                @pl.when(h == 0)
+    def rs_event(n, h, cut):
+        for way in (0, 1):
+            @pl.when(h == 0)
+            def _():
+                @pl.when(n >= R_SLOTS)
                 def _():
-                    @pl.when(n >= R_SLOTS)
-                    def _():
-                        pl.semaphore_wait(credit.at[way], 1)
-
-                    rs_copy(n, way, 0).start()
-
-                @pl.when((h > 0) & (h <= hops(n, way)))
+                    pl.semaphore_wait(credit.at[way], 1)
+
+                rs_copy(n, way, 0, cut).start()
+
+            @pl.when((h > 0) & (h <= hops(n, way)))
+            def _():
+                rs_copy(n, way, h - 1, cut).wait_recv()
+
+                @pl.when(h < hops(n, way))
                 def _():
-                    rs_copy(n, way, h - 1).wait_recv()
-
-                    @pl.when(h < hops(n, way))
-                    def _():
-                        step = hops(n, way) - h
-                        own = chip_at(q + step if way == 0 else q - step)
-                        total = W[slot, own].astype(F32) + R[came(n, way, h - 1)].astype(F32)
-                        W[slot, own] = total.astype(BF16)
-                        rs_copy(n, way, h).start()
-
-            @pl.when(h == 4)
-            def _():
-                total = W[slot, chip].astype(F32) + R[came(n, 0, hops(n, 0) - 1)].astype(F32)
-                total = total + R[came(n, 1, hops(n, 1) - 1)].astype(F32)
-                W[slot, chip] = total.astype(BF16)
-
-                @pl.when(kind(n) == 2)
+                    step = hops(n, way) - h
+                    own = spot(n, chip_at(q + step if way == 0 else q - step), cut)
+                    total = W[own].astype(F32) + R[came(n, way, h - 1, cut)].astype(F32)
+                    W[own] = total.astype(BF16)
+                    rs_copy(n, way, h, cut).start()
+
+        @pl.when(h == 4)
+        def _():
+            own = spot(n, chip, cut)
+            total = W[own].astype(F32) + R[came(n, 0, hops(n, 0) - 1, cut)].astype(F32)
+            total = total + R[came(n, 1, hops(n, 1) - 1, cut)].astype(F32)
+            W[own] = total.astype(BF16)
+            if cut:
+                out_down(n, cut).start()
+                return
+
+            @pl.when(kind(n) == 2)
+            def _():
+                out_down(n, cut).start()
+
+            @pl.when(kind(n) != 2)
+            def _():
+                out_here(n).start()
+                out_there(n).start()
+
+            @pl.when(n <= ALL - R_SLOTS)
+            def _():
+                for way in (0, 1):
+                    pl.semaphore_signal(credit.at[way], inc=1, device_id=ring[1 - way], device_id_type=MESH)
+
+    def rs_events(lo, hi, end=False):
+        def body(e):
+            h = lax.rem(4 * e, 5)
+            n = (e - 4 * h) // 5
+
+            @pl.when((n >= 0) & (n < ALL - 1))
+            def _():
+                rs_event(n, h, False)
+
+            if end:
+                @pl.when((n >= ALL - 1) & (n <= ALL))
                 def _():
-                    out_down(n).start()
-
-                @pl.when(kind(n) != 2)
-                def _():
-                    out_here(n).start()
-                    out_there(n).start()
-
-                @pl.when(n < ALL - R_SLOTS)
-                def _():
-                    for way in (0, 1):
-                        pl.semaphore_signal(credit.at[way], inc=1, device_id=ring[1 - way], device_id_type=MESH)
-
-    def rs_events(lo, hi):
-        def body(e, _):
-            h = lax.rem(4 * e, 5)
-            rs_event((e - 4 * h) // 5, h)
-            return 0
-
-        lax.fori_loop(lo, hi, body, 0)
+                    rs_event(n, h, True)
+
+        loop(hi, body, lo)
 
     block = min(256, tok)
     blocks = 2 * tok // block
@@ -360,34 +379,34 @@
         wide = h.astype(F32)
         return (wide * lax.rsqrt(jnp.mean(wide * wide, -1, keepdims=True) + 1e-6)).astype(BF16)
 
+    def block_of(c, t):
+        return pl.ds(pl.multiple_of(c * tok + t * block, block), block)
+
     def norm_block(c, flip):
-        def body(t, _):
-            s = pl.ds(pl.multiple_of(c * tok + t * block, block), block)
+        def body(t):
+            s = block_of(c, t)
             a = normed(A[s, :])
             A[s, :] = a
             if flip:
                 AT[:, s] = a.T
-            return 0
-
-        lax.fori_loop(0, tok // block, body, 0)
+
+        loop(tok // block, body)
 
     def flip_dy(c):
-        def body(t, _):
-            s = pl.ds(pl.multiple_of(c * tok + t * block, block), block)
+        def body(t):
+            s = block_of(c, t)
             DYT[:, s] = DY[s, :].T
-            return 0
-
-        lax.fori_loop(0, tok // block, body, 0)
+
+        loop(tok // block, body)
 
     def clear():
-        def body(t, _):
+        def body(t):
             ACC[part(t), :] = jnp.zeros((block, d), F32)
-            return 0
-
-        lax.fori_loop(0, blocks, body, 0)
+
+        loop(blocks, body)
 
     def own_block(t):
-        return pl.ds(pl.multiple_of(core * tok + t * block, block), block)
+        return block_of(core, t)
 
     def nth(t):
         return part(lax.rem(t + 2 * (1 - core), 4), tile)
@@ -400,7 +419,7 @@
         i, hh = j // 2, lax.rem(j, 2)
         r = 3 * i + 1 + hh
 
-        def body(t, _):
+        def body(t):
             s = nth(t)
             at = A[s, :]
             gate = nn(at, W[r, :, 0].reshape(d, -1))
@@ -413,9 +432,8 @@
                 swap(0, t).start()
 
             after(t)
-            return 0
-
-        lax.fori_loop(0, 4, body, 0)
+
+        loop(4, body)
 
     ag_events(0, 1)
     prep_all(3, ROUNDS)
@@ -436,7 +454,7 @@
     flip_dy(1 - core)
     ag_events(11, FIRST[0])
 
-    def first(j, _):
+    def first(j):
         i, hh = j // 2, lax.rem(j, 2)
 
         @pl.when(hh == 0)
@@ -446,9 +464,8 @@
         ag_ready(3 * i + 1 + hh)
         lo, count = pick(FIRST[:8], j), pick(FIRST[1:], j) - pick(FIRST[:8], j)
         forward(j, lambda t: ag_events(lo + (count * t) // 4, lo + (count * (t + 1)) // 4))
-        return 0
-
-    lax.fori_loop(0, 8, first, 0)
+
+    loop(8, first)
 
     whole = DG.at[pl.ds(0, 4 * ALL // 3 * rows)]
     remote(whole, whole, prep_send, prep_rem.at[0], mate).wait_send()
@@ -459,14 +476,13 @@
     swap(0, 0).wait()
     swap(0, 1).wait()
 
-    def residual(t, _):
+    def residual(t):
         mlp = (ACC[own_block(t), :] + PT[part(t), :]).astype(BF16)
         h = (DG[part(t), :].astype(F32) + mlp.astype(F32)).astype(BF16)
         ACT[part(t), :] = h
         A[own_block(t), :] = h
-        return 0
-
-    lax.fori_loop(0, tok // block, residual, 0)
+
+    loop(tok // block, residual)
     h1 = ACT.at[pl.ds(0, tok)]
     send_h = remote(h1, A.at[mine], ex_send.at[3], ex_recv.at[3], mate)
     keep_h = pltpu.make_async_copy(h1, h1_ref, loc.at[3])
@@ -488,7 +504,7 @@
         by_h = (by_a * scale - wide * (scale * scale * scale * along)).astype(BF16)
         return (DY[own_block(t), :].astype(F32) + by_h.astype(F32)).astype(BF16)
 
-    def chunk(c, _):
+    def chunk(c):
         l = 1 - c // 8
         j = lax.rem(c, 8)
         i, hh = turn(l, j // 2), lax.rem(j, 2)
@@ -499,9 +515,10 @@
         lo = jnp.where(c == 8, BETWEEN[1], events_by(c))
         count = events_by(c + 1) - lo
 
+        ag_lo, ag_count = pick(SECOND[:-1], c), pick((*SECOND[1:], LAST_AG), c) - pick(SECOND[:-1], c)
+
         def serve(slot):
-            ag_lo, ag_hi = 62 + 8 * c + slot, 63 + 8 * c + slot
-            ag_events(jnp.minimum(ag_lo, LAST_AG), jnp.minimum(ag_hi, LAST_AG))
+            ag_events(ag_lo + (ag_count * slot) // 8, ag_lo + (ag_count * slot + ag_count) // 8)
             rs_events(lo + (count * slot) // 8, lo + (count * slot + count) // 8)
 
         @pl.when(c == 8)
@@ -519,13 +536,12 @@
             swap(1, 0).wait()
             swap(1, 1).wait()
 
-            def body(t, _):
+            def body(t):
                 dh = norm_back(DG, t)
                 DY[own_block(t), :] = dh
                 ACT[part(t), :] = dh
-                return 0
-
-            lax.fori_loop(0, tok // block, body, 0)
+
+            loop(tok // block, body)
             send = remote(ACT.at[pl.ds(0, tok)], DY.at[mine], ex_send.at[4], ex_recv.at[4], mate)
             send.start()
             clear()
@@ -540,11 +556,10 @@
             send.wait()
             flip_dy(1 - core)
 
-            def gone(g, _):
+            def gone(g):
                 ag_retire(g)
-                return 0
-
-            lax.fori_loop(GATHERED - S_SLOTS, GATHERED, gone, 0)
+
+            loop(GATHERED, gone, GATHERED - S_SLOTS)
             across_sent(1)
 
         @pl.when(l == 1)
@@ -555,7 +570,7 @@
 
             ag_ready(base + 1 + hh)
 
-        def tokens(t, _):
+        def tokens(t):
             s = nth(t)
             at = A[s, :]
             wg, wu = W[base + 1 + hh, :, 0].reshape(d, -1), W[base + 1 + hh, :, 1].reshape(d, -1)
@@ -575,9 +590,8 @@
                 swap(2 - l, t).start()
 
             serve(t)
-            return 0
-
-        lax.fori_loop(0, 4, tokens, 0)
+
+        loop(4, tokens)
 
         for back, when in ((0, 0), (1, 1), (2, 0)):
             n = 3 * pair + back - T_SLOTS
@@ -586,14 +600,13 @@
             def _():
                 rs_retire(n)
 
-        def grads_up(p, _):
+        def grads_up(p):
             s = pl.ds(pl.multiple_of(p * (d // 2), d // 2), d // 2)
             W[up_slot, pl.ds(4 * p, 4), 0] = nn(AT[s, :], DG[...]).astype(BF16).reshape(4, half, -1)
             W[up_slot, pl.ds(4 * p, 4), 1] = nn(AT[s, :], DU[...]).astype(BF16).reshape(4, half, -1)
             serve(4 + p)
-            return 0
-
-        lax.fori_loop(0, 2, grads_up, 0)
+
+        loop(2, grads_up)
 
         for p in range(2):
             s = slice(p * (d // 2), (p + 1) * (d // 2))
@@ -601,9 +614,7 @@
             W[down_slot, pl.ds(4 * hh, 4), :, :, s] = g.reshape(4, 2, half, d // 2)
             serve(6 + p)
 
-        return 0
-
-    lax.fori_loop(0, 16, chunk, 0)
+    loop(16, chunk)
 
     fetch = pltpu.make_async_copy(x_ref, DG.at[pl.ds(0, tok)], loc.at[7])
     fetch.start()
@@ -612,61 +623,59 @@
     swap(2, 0).wait()
     swap(2, 1).wait()
 
-    def last(t, _):
+    def last(t):
         ACT[part(t), :] = norm_back(DG, t)
-        return 0
-
-    lax.fori_loop(0, tok // block, last, 0)
+
+    loop(tok // block, last)
     put = pltpu.make_async_copy(ACT.at[pl.ds(0, tok)], dx_ref, loc.at[8])
     put.start()
-    rs_events(111, LAST_RS)
+    rs_retire(ALL - T_SLOTS)
+    rs_events(111, LAST_RS, True)
 
     put.wait()
     for copy in (send_x, send_xp, send_dy):
         copy.wait_send()
 
-    def sent(r, _):
-        @pl.when(r >= ALL - T_SLOTS)
-        def _():
-            rs_retire(r)
-
-        @pl.when(kind(r) != 2)
-        def _():
-            out_there(r).wait_recv()
-
-        return 0
-
+    def sent(n):
+        rs_retire(n)
+
+    for n in (ALL - 1, ALL):
+        rs_retire(jnp.int32(n), True)
     across_sent(0)
-    lax.fori_loop(0, ALL, sent, 0)
+    loop(ALL - 1, sent, ALL - T_SLOTS + 1)
+    ups = W.at[0]
+    remote(ups, ups, out_send.at[0], out_recv, mate).wait_recv()
 
 
 def put_kernel(dx_ref, og_ref, od_ref, dx_out, dwg_out, dwu_out, dwd_out, dx, og, od, dwg, dwu, came, went):
-    layers = dwg.shape[0]
-    strip = dwg.shape[2] // 64
-    loads = [pltpu.make_async_copy(og_ref.at[l], og.at[l], came.at[l]) for l in range(layers)]
-    others = [(dx_ref, dx, dx_out), (od_ref, od, dwd_out)]
+    layers, _, ff = dwg.shape
+    strip = ff // 64
+
+    def copies(pairs, sems):
+        return [pltpu.make_async_copy(src, dst, sems.at[k]) for k, (src, dst) in enumerate(pairs)]
+
+    each = range(layers)
+    loads = copies([(dx_ref, dx), (od_ref, od)] + [(og_ref.at[l], og.at[l]) for l in each], came)
+    stores = [(dx, dx_out), (od, dwd_out)]
+    stores = copies(stores + [(a.at[l], b.at[l]) for l in each for a, b in ((dwg, dwg_out), (dwu, dwu_out))], went)
+    first = loads[:layers], stores[:layers]
     for copy in loads:
         copy.start()
-    for k, (src, buffer, _) in enumerate(others):
-        pltpu.make_async_copy(src, buffer, came.at[2 + k]).start()
-    for l in range(layers):
-        loads[l].wait()
+    for load, store in zip(*first, strict=True):
+        load.wait()
+        store.start()
+    for l in each:
+        loads[layers + l].wait()
         for part in range(16):
             c, i, hh = part // 8, part // 2 % 4, part % 2
             for s in range(4):
                 column = strip * (8 * (4 * hh + s) + 4 * c + i)
                 for g, out in enumerate((dwg, dwu)):
                     out[l, :, column : column + strip] = og[l, c, i, hh, g, :, strip * s : strip * (s + 1)]
-        pltpu.make_async_copy(dwg.at[l], dwg_out.at[l], went.at[2 * l]).start()
-        pltpu.make_async_copy(dwu.at[l], dwu_out.at[l], went.at[2 * l + 1]).start()
-    for k, (src, buffer, dst) in enumerate(others):
-        pltpu.make_async_copy(src, buffer, came.at[2 + k]).wait()
-        pltpu.make_async_copy(buffer, dst, went.at[4 + k]).start()
-    for l in range(layers):
-        pltpu.make_async_copy(dwg.at[l], dwg_out.at[l], went.at[2 * l]).wait()
-        pltpu.make_async_copy(dwu.at[l], dwu_out.at[l], went.at[2 * l + 1]).wait()
-    for k, (_, buffer, dst) in enumerate(others):
-        pltpu.make_async_copy(buffer, dst, went.at[4 + k]).wait()
+        for store in stores[2 * (l + 1) : 2 * (l + 2)]:
+            store.start()
+    for store in stores:
+        store.wait()
 
 
 def of_a_device(x, dy, w_gate, w_up, w_down):
@@ -708,12 +717,12 @@
             dma((S_SLOTS, 2)),
             dma((S_SLOTS, 2, 4)),
             dma((2,)),
-            dma((ALL,)),
+            dma((10,)),
             dma((T_SLOTS, 2)),
             dma((R_SLOTS, 2, 4)),
             dma((T_SLOTS,)),
             dma((T_SLOTS,)),
-            dma((2 * ALL // 3,)),
+            dma(()),
             dma((5,)),
             dma((5,)),
             dma((3, 2)),

time: 403 us -> 401 us (level)
  no operation moved by 1% of the time
where the time goes in v4:
time: 401 us
  Pallas kernels  400 us (100%)
    pallas_call x1, Pallas kernels, of_a_device(): pl.pallas_call(functools.partial(kernel, tile), out_shape=tuple((jax.Shap...  396 us

profile of v4, /device:TPU:0, one launch (start us, length us, event | category | flops | bytes accessed | tf_op | source)
XLA Modules:
  0.0 400.5 jit_solution(13756873901586847617)
XLA Ops:
  0.6 396.3 %shard_map.84 = (bf16[1024,512]{1,0:T(8,128)(2,1)}, bf16[2,2,4,2,2,32,512]{6,5,4,3,2,1,0:T(8,128)(2,1)}, bf16[2,4,2,64,512]{4,3,2,1,0:T(8,128)(2,1)}, bf16[1024,512]{1,0:T(8,128)(2,1)}, bf16[1024,512]{1,0:T(8,128)(2,1)}) custom-call(bf16[1024,512]{1,0:T(8,128)(2,1)} %bitcast.5, bf16[1024,512]{1,0:T(8,128)(2,1)} %bitcast.6, bf16[2,32,8192]{2,1,0:T(8,128)(2,1)} %wg_ref.1, ...), custom_call_target="tpu_custom_call" | custom-call | tf_op jit(solution)/shard_map/pallas_call | solution.py:693
  397.0 3.6 shard_map.85

commit v5 on v4

--- a/solution.py
+++ b/solution.py
@@ -11,7 +11,7 @@
 F32, BF16 = jnp.float32, jnp.bfloat16
 ROUNDS = 12
 ALL = 2 * ROUNDS
-T_SLOTS, R_SLOTS, S_SLOTS = 8, 6, 8
+T_SLOTS, R_SLOTS, S_SLOTS = 8, 6, 6
 GATHERED = 14
 FIRST = (21, 27, 31, 37, 41, 47, 50, 52, 55)
 BETWEEN = 45, 51
@@ -411,9 +411,9 @@
     def nth(t):
         return part(lax.rem(t + 2 * (1 - core), 4), tile)
 
-    def swap(k, t):
+    def swap(t):
         src = ACC.at[pl.ds(pl.multiple_of((1 - core) * tok + t * tile, tile), tile)]
-        return remote(src, PT.at[part(t, tile)], sw_send.at[k, t], sw_recv.at[k, t], mate)
+        return remote(src, PT.at[part(t, tile)], sw_send.at[t], sw_recv.at[t], mate)
 
     def forward(j, after):
         i, hh = j // 2, lax.rem(j, 2)
@@ -429,7 +429,7 @@
 
             @pl.when((j == 7) & (t < 2))
             def _():
-                swap(0, t).start()
+                swap(t).start()
 
             after(t)
 
@@ -469,12 +469,12 @@
 
     whole = DG.at[pl.ds(0, 4 * ALL // 3 * rows)]
     remote(whole, whole, prep_send, prep_rem.at[0], mate).wait_send()
-    fetch = pltpu.make_async_copy(x_ref, DG.at[pl.ds(0, tok)], loc.at[2])
+    fetch = pltpu.make_async_copy(x_ref, DG.at[pl.ds(0, tok)], loc.at[0])
     fetch.start()
     ag_events(55, 57)
     fetch.wait()
-    swap(0, 0).wait()
-    swap(0, 1).wait()
+    swap(0).wait()
+    swap(1).wait()
 
     def residual(t):
         mlp = (ACC[own_block(t), :] + PT[part(t), :]).astype(BF16)
@@ -485,7 +485,7 @@
     loop(tok // block, residual)
     h1 = ACT.at[pl.ds(0, tok)]
     send_h = remote(h1, A.at[mine], ex_send.at[3], ex_recv.at[3], mate)
-    keep_h = pltpu.make_async_copy(h1, h1_ref, loc.at[3])
+    keep_h = pltpu.make_async_copy(h1, h1_ref, loc.at[1])
     send_h.start()
     keep_h.start()
     clear()
@@ -519,22 +519,22 @@
 
         def serve(slot):
             ag_events(ag_lo + (ag_count * slot) // 8, ag_lo + (ag_count * slot + ag_count) // 8)
-            rs_events(lo + (count * slot) // 8, lo + (count * slot + count) // 8)
+            rs_events(lo + (count * slot + 2) // 8, lo + (count * slot + count + 2) // 8)
 
         @pl.when(c == 8)
         def _():
             start, end = BETWEEN
-            again = pltpu.make_async_copy(x_ref, A.at[mine], loc.at[5])
+            again = pltpu.make_async_copy(x_ref, A.at[mine], loc.at[1])
             again.start()
             send_xp.wait_recv()
-            other = pltpu.make_async_copy(xp_ref, A.at[theirs], loc.at[6])
+            other = pltpu.make_async_copy(xp_ref, A.at[theirs], loc.at[2])
             other.start()
-            fetch = pltpu.make_async_copy(h1_ref, DG.at[pl.ds(0, tok)], loc.at[4])
+            fetch = pltpu.make_async_copy(h1_ref, DG.at[pl.ds(0, tok)], loc.at[0])
             fetch.start()
             rs_events(start, start + 1)
             fetch.wait()
-            swap(1, 0).wait()
-            swap(1, 1).wait()
+            swap(0).wait()
+            swap(1).wait()
 
             def body(t):
                 dh = norm_back(DG, t)
@@ -587,7 +587,7 @@
 
             @pl.when((j == 7) & (t < 2))
             def _():
-                swap(2 - l, t).start()
+                swap(t).start()
 
             serve(t)
 
@@ -616,18 +616,18 @@
 
     loop(16, chunk)
 
-    fetch = pltpu.make_async_copy(x_ref, DG.at[pl.ds(0, tok)], loc.at[7])
+    fetch = pltpu.make_async_copy(x_ref, DG.at[pl.ds(0, tok)], loc.at[0])
     fetch.start()
     rs_events(110, 111)
     fetch.wait()
-    swap(2, 0).wait()
-    swap(2, 1).wait()
+    swap(0).wait()
+    swap(1).wait()
 
     def last(t):
         ACT[part(t), :] = norm_back(DG, t)
 
     loop(tok // block, last)
-    put = pltpu.make_async_copy(ACT.at[pl.ds(0, tok)], dx_ref, loc.at[8])
+    put = pltpu.make_async_copy(ACT.at[pl.ds(0, tok)], dx_ref, loc.at[1])
     put.start()
     rs_retire(ALL - T_SLOTS)
     rs_events(111, LAST_RS, True)
@@ -725,9 +725,9 @@
             dma(()),
             dma((5,)),
             dma((5,)),
-            dma((3, 2)),
-            dma((3, 2)),
-            dma((9,)),
+            dma((2,)),
+            dma((2,)),
+            dma((3,)),
             pltpu.SemaphoreType.REGULAR((2,)),
         ],
         compiler_params=pltpu.CompilerParams(

time: 401 us -> 400 us (level)
  no operation moved by 1% of the time
where the time goes in v5:
time: 400 us
  Pallas kernels  399 us (100%)
    pallas_call x1, Pallas kernels, of_a_device(): pl.pallas_call(functools.partial(kernel, tile), out_shape=tuple((jax.Shap...  395 us

profile of v5, /device:TPU:0, one launch (start us, length us, event | category | flops | bytes accessed | tf_op | source)
XLA Modules:
  0.0 399.6 jit_solution(2782953351875903439)
XLA Ops:
  0.6 395.4 %shard_map.84 = (bf16[1024,512]{1,0:T(8,128)(2,1)}, bf16[2,2,4,2,2,32,512]{6,5,4,3,2,1,0:T(8,128)(2,1)}, bf16[2,4,2,64,512]{4,3,2,1,0:T(8,128)(2,1)}, bf16[1024,512]{1,0:T(8,128)(2,1)}, bf16[1024,512]{1,0:T(8,128)(2,1)}) custom-call(bf16[1024,512]{1,0:T(8,128)(2,1)} %bitcast.5, bf16[1024,512]{1,0:T(8,128)(2,1)} %bitcast.6, bf16[2,32,8192]{2,1,0:T(8,128)(2,1)} %wg_ref.1, ...), custom_call_target="tpu_custom_call" | custom-call | tf_op jit(solution)/shard_map/pallas_call | solution.py:693
  396.1 3.6 shard_map.85

commit v6 on v5

--- a/solution.py
+++ b/solution.py
@@ -13,7 +13,7 @@
 ALL = 2 * ROUNDS
 T_SLOTS, R_SLOTS, S_SLOTS = 8, 6, 6
 GATHERED = 14
-FIRST = (21, 27, 31, 37, 41, 47, 50, 52, 55)
+FIRST = (25, 28, 31, 37, 41, 47, 50, 52, 55)
 BETWEEN = 45, 51
 SECOND = (62, 67, 77, 82, 82)
 LAST_AG, LAST_RS = 5 * (GATHERED - 1) + 17, 5 * ALL + 17

time: 400 us -> 400 us (level)
  no operation moved by 1% of the time
where the time goes in v6:
time: 400 us; the launch traced here: 399 us
  Pallas kernels  399 us (100%)
    pallas_call x1, Pallas kernels, of_a_device(): pl.pallas_call(functools.partial(kernel, tile), out_shape=tuple((jax.Shap...  395 us

profile of v6, /device:TPU:0, one launch (start us, length us, event | category | flops | bytes accessed | tf_op | source)
XLA Modules:
  0.0 399.3 jit_solution(14467210340773956021)
XLA Ops:
  0.6 395.1 %shard_map.84 = (bf16[1024,512]{1,0:T(8,128)(2,1)}, bf16[2,2,4,2,2,32,512]{6,5,4,3,2,1,0:T(8,128)(2,1)}, bf16[2,4,2,64,512]{4,3,2,1,0:T(8,128)(2,1)}, bf16[1024,512]{1,0:T(8,128)(2,1)}, bf16[1024,512]{1,0:T(8,128)(2,1)}) custom-call(bf16[1024,512]{1,0:T(8,128)(2,1)} %bitcast.5, bf16[1024,512]{1,0:T(8,128)(2,1)} %bitcast.6, bf16[2,32,8192]{2,1,0:T(8,128)(2,1)} %wg_ref.1, ...), custom_call_target="tpu_custom_call" | custom-call | tf_op jit(solution)/shard_map/pallas_call | solution.py:693
  395.8 3.6 shard_map.85
